TPU v7x, 32 devices: a whole 2x2x4 slice. The times are simulated.
32 devices in a mesh: tm: 16 (over z, x, core), grp: 2 (over y).
Axes of the slice: x: 2, y: 2, z: 4, core: 2. Of those that a mesh axis runs over, the one named last changes fastest.
Arguments:
- residual: float32 [16, 2, 3072], P('tm', 'grp'), may hold values from -6 to 6
- weight: float32 [16, 2, 3072], P('tm', 'grp'), may hold values from 0.25 to 4
- source_part: float32 [5, 16, 2, 3072], P(None, 'tm', 'grp'), may hold values from -2.5 to 2.5
- source_index: int32 [16, 2, 3072], P('tm', 'grp'), may hold values from 0 to 4095
- source_delta: float32 [5, 16, 4096], P(None, 'tm'), may hold values from -6 to 6
- attitude_part: float32 [3, 16, 2, 3072], P(None, 'tm', 'grp'), may hold values from -6 to 6
- spline_phase: float32 [16, 2, 3072], P('tm', 'grp'), may hold values from 0 to 1
- knot_index: int32 [16, 2, 3072], P('tm', 'grp'), may hold values from 0 to 1535, as said below
- calib_part: float32 [6, 16, 2, 3072], P(None, 'tm', 'grp'), may hold values from -6 to 6
- calib_index: int32 [16, 2, 3072], P('tm', 'grp'), may hold values from 0 to 2047
- global_part: float32 [4, 16, 2, 3072], P(None, 'tm', 'grp'), may hold values from -6 to 6
Outputs:
- residual_new: float32 [16, 2, 3072], P('tm', 'grp')
- attitude_step: float32 [3, 1536], P(None, 'tm')
- calib_step: float32 [6, 2048], replicated
- global_step: float32 [4], replicated
Inputs may be any that keep to these rules, and one draw needn't show every extreme that they name: `knot_index`: observation r of interval t (in any group) lies in knot interval t * 96 + 4 * (r // 128) + j for some j in 0 .. 3.
All inputs are finite; a program needn't handle non-finite values.
Results may differ from a plain program's by a relative error of at most 0.00012.
Values sent between devices are 32-bit elements; how exact they have to be, the bound alone decides.
A program may use at most 128 MiB of HBM per device.

v0:
```python
import functools

import jax
import jax.numpy as jnp
from jax import lax
from jax.experimental import pallas as pl
from jax.experimental.pallas import tpu as pltpu
from jax.sharding import PartitionSpec as P

TILE = 128
KPT = 4
UNITS = 2048
CPAR = 6
GPAR = 4
ATT_SWEEPS = 4

OMEGA = 0.6
RIDGE = 1.0
LANES = 128
LOW = 256
HALO = 3 * ATT_SWEEPS
MESH = pl.DeviceIdType.MESH
F32 = jnp.float32
BF16 = jnp.bfloat16

ATT_ROWS = 72
UNIT_ROWS = 24
NORMAL_ROWS = 32


def pairs_of(extent):
    return [(a, b) for a in range(extent) for b in range(a, extent)]


def lane_pick(table, index):
    return lax.gather(
        table,
        index[..., None],
        lax.GatherDimensionNumbers(
            offset_dims=(),
            collapsed_slice_dims=(1,),
            start_index_map=(1,),
            operand_batching_dims=(0,),
            start_indices_batching_dims=(0,),
        ),
        (1, 1),
        mode=lax.GatherScatterMode.PROMISE_IN_BOUNDS,
    )


def spline_basis(phase):
    inverse = 1.0 - phase
    square = phase * phase
    cubed = square * phase
    return [
        inverse * inverse * inverse / 6.0,
        (3.0 * cubed - 6.0 * square + 4.0) / 6.0,
        (-3.0 * cubed + 3.0 * square + 3.0 * phase + 1.0) / 6.0,
        cubed / 6.0,
    ]


def cholesky_lists(matrix, extent):
    lower = [[None] * extent for _ in range(extent)]
    inverse = [None] * extent
    for column in range(extent):
        pivot = matrix[column][column]
        for k in range(column):
            pivot = pivot - lower[column][k] * lower[column][k]
        root = jnp.sqrt(pivot)
        lower[column][column] = root
        inverse[column] = 1.0 / root
        for row in range(column + 1, extent):
            entry = matrix[row][column]
            for k in range(column):
                entry = entry - lower[row][k] * lower[column][k]
            lower[row][column] = entry * inverse[column]
    return lower, inverse


def solve_lower(lower, inverse, vector):
    result = []
    for row in range(len(vector)):
        running = vector[row]
        for k in range(row):
            running = running - lower[row][k] * result[k]
        result.append(running * inverse[row])
    return result


def solve_upper(lower, inverse, vector):
    extent = len(vector)
    result = [None] * extent
    for row in reversed(range(extent)):
        running = vector[row]
        for k in range(row + 1, extent):
            running = running - lower[k][row] * result[k]
        result[row] = running * inverse[row]
    return result


def symmetric(upper, extent):
    matrix = [[None] * extent for _ in range(extent)]
    for position, (a, b) in enumerate(pairs_of(extent)):
        value = upper[position] + (RIDGE if a == b else 0.0)
        matrix[a][b] = value
        matrix[b][a] = value
    return matrix


def split_three(value):
    first = value.astype(BF16).astype(F32)
    rest = value - first
    second = rest.astype(BF16).astype(F32)
    third = (rest - second).astype(BF16).astype(F32)
    return [first, second, third]


def dot_nt(left, right):
    return lax.dot_general(
        left, right, (((1,), (1,)), ((), ())), preferred_element_type=F32
    )


def two_tiles(ref, tile, rows, tiles):
    return jnp.concatenate(
        [ref[pl.ds(tile, rows, stride=tiles), :], ref[pl.ds(tile + 1, rows, stride=tiles), :]],
        axis=1,
    )


def two_rows(ref, tile):
    return jnp.concatenate([ref[pl.ds(tile, 1), :], ref[pl.ds(tile + 1, 1), :]], axis=1)


def one_hot(row, extent):
    spots = lax.broadcasted_iota(jnp.int32, (extent, row.shape[1]), 0)
    return jnp.where(spots == row, 1.0, 0.0).astype(BF16)


def by_high(part, high):
    return jnp.concatenate(
        [jnp.where(high == h, part, 0.0) for h in range(UNITS // LOW)], axis=0
    )


def block_pieces(blocks):
    width = UNITS // blocks
    for piece in range(UNITS // LANES):
        unit = piece * LANES
        yield unit // width, unit % width, unit // LOW, unit % LOW


def step_kernel(
    shape, nodes_dev, res_ref, w_ref, sp_ref, si_ref, sd_ref, ap_ref, ph_ref, kn_ref, cp_ref,
    ci_ref, gp_ref, second_ref, step_ref, out_ref, glob_ref,
    att, cal, rcal, acc_att, acc_cal, acc_rhs, normal_ref, mats_ref, rhs_ref,
    near, mine, whole, rwhole, rmine, ready, spread,
    near_s, near_r, mine_s, mine_r, whole_s, whole_r,
    rwhole_s, rwhole_r, rmine_s, rmine_r, spread_s, spread_r,
):
    count, groups, blocks = shape
    t, g = lax.axis_index("tm"), lax.axis_index("grp")
    has_before, has_after = t > 0, t < count - 1

    def peer_tm(k):
        return lax.rem(t + k, count)

    def peer_grp(k):
        return lax.rem(g + k, groups)

    barrier = pltpu.get_barrier_semaphore()

    def greet(where):
        pl.semaphore_signal(barrier, inc=1, device_id=where, device_id_type=MESH)

    lax.fori_loop(1, count, lambda k, c: (greet({"tm": peer_tm(k), "grp": g}), c)[1], 0)
    for k in range(1, groups):
        greet({"tm": t, "grp": peer_grp(k)})
        greet({"tm": peer_tm(1), "grp": peer_grp(k)})
        greet({"tm": peer_tm(count - 1), "grp": peer_grp(k)})
    tiles = res_ref.shape[0]
    weights = w_ref[...]
    sources = si_ref[...]
    high, low = lax.shift_right_logical(sources, 7), lax.bitwise_and(sources, 127)
    picked = [jnp.zeros((tiles, LANES), F32) for _ in range(5)]
    for row in range(sd_ref.shape[1]):
        here = high == row
        for c in range(5):
            table = jnp.broadcast_to(sd_ref[c, row : row + 1, :], (tiles, LANES))
            picked[c] = jnp.where(here, lane_pick(table, low), picked[c])
    total = sp_ref[0] * picked[0]
    for c in range(1, 5):
        total = total + sp_ref[c] * picked[c]
    first = res_ref[...] - total
    basis = spline_basis(ph_ref[...])
    axes = [ap_ref[c] for c in range(3)]
    products = [weights * axes[a] * axes[b] for a, b in pairs_of(3)]
    rights = [weights * axes[a] * first for a in range(3)]
    place = 0
    for i in range(4):
        for d in range(4 - i):
            both = basis[i] * basis[i + d]
            for product in products:
                att[place * tiles : (place + 1) * tiles, :] = both * product
                place += 1
    for i in range(4):
        for right in rights:
            att[place * tiles : (place + 1) * tiles, :] = basis[i] * right
            place += 1
    acc_att[...] = jnp.zeros_like(acc_att)
    base = lax.axis_index("tm") * (tiles * KPT)

    def bin_nodes(no, carry):
        tile = no * 2
        knots = two_rows(kn_ref, tile) - base
        nodes = one_hot(knots, LANES)
        part = acc_att[...]
        for piece in split_three(two_tiles(att, tile, ATT_ROWS, tiles)):
            part = part + dot_nt(piece.astype(BF16), nodes)
        acc_att[...] = part
        return carry

    lax.fori_loop(0, tiles // 2, bin_nodes, 0, unroll=6)
    band = [None] * 5
    place = 0
    for i in range(4):
        for d in list(range(4 - i)):
            rows = acc_att[place : place + 6, :]
            rows = pltpu.roll(rows, i, 1) if i else rows
            band[d] = rows if band[d] is None else band[d] + rows
            place += 6
    for i in range(4):
        rows = acc_att[place : place + 3, :]
        rows = pltpu.roll(rows, i, 1) if i else rows
        band[4] = rows if band[4] is None else band[4] + rows
        place += 3
    for d in range(4):
        normal_ref[d * 6 : (d + 1) * 6, :] = band[d]
    normal_ref[24:27, :] = band[4]
    normal_ref[27:, :] = jnp.zeros((NORMAL_ROWS - 27, LANES), F32)
    pl.semaphore_wait(barrier, count - 1 + 3 * (groups - 1))

    def near_copy(offset, k):
        slot = (1 - offset) * groups + g
        return pltpu.make_async_remote_copy(
            src_ref=normal_ref,
            dst_ref=near.at[slot],
            send_sem=near_s.at[(offset + 1) * groups + k],
            recv_sem=near_r.at[slot],
            device_id={"tm": t + offset, "grp": peer_grp(k)},
            device_id_type=MESH,
        )

    def near_arrival(offset, k):
        slot = (offset + 1) * groups + peer_grp(k)
        return pltpu.make_async_remote_copy(
            src_ref=normal_ref,
            dst_ref=near.at[slot],
            send_sem=near_s.at[(offset + 1) * groups + k],
            recv_sem=near_r.at[slot],
            device_id={"tm": t + offset, "grp": peer_grp(k)},
            device_id_type=MESH,
        )

    def each_near(do):
        for k in range(1, groups):
            do(0, k)

        @pl.when(has_before)
        def _():
            for k in range(groups):
                do(-1, k)

        @pl.when(has_after)
        def _():
            for k in range(groups):
                do(1, k)

    each_near(lambda offset, k: near_copy(offset, k).start())

    place = 0
    for a, b in pairs_of(CPAR):
        cal[place * tiles : (place + 1) * tiles, :] = weights * cp_ref[a] * cp_ref[b]
        place += 1
    cal[place * tiles :, :] = jnp.zeros(((UNIT_ROWS - place) * tiles, LANES), F32)
    global_rows = [
        jnp.sum(weights * gp_ref[a] * gp_ref[b], axis=0, keepdims=True)
        for a, b in pairs_of(GPAR)
    ]
    acc_cal[...] = jnp.zeros_like(acc_cal)

    def bin_units(no, carry):
        tile = no * 2
        units = two_rows(ci_ref, tile)
        upper, lower = lax.shift_right_logical(units, 8), lax.bitwise_and(units, 255)
        spots = one_hot(lower, LOW)
        part = acc_cal[...]
        for piece in split_three(two_tiles(cal, tile, UNIT_ROWS, tiles)):
            part = part + dot_nt(by_high(piece, upper).astype(BF16), spots)
        acc_cal[...] = part
        return carry

    lax.fori_loop(0, tiles // 2, bin_units, 0, unroll=6)
    mats_ref[...] = jnp.zeros_like(mats_ref)
    for block, at, h, start in block_pieces(blocks):
        mats_ref[block, 0:21, at : at + LANES] = acc_cal[
            h * UNIT_ROWS : h * UNIT_ROWS + 21, start : start + LANES
        ]
        if at == 0:
            for no, row in enumerate(global_rows):
                mats_ref[block, 21 + no : 22 + no, 0:LANES] = row

    def whole_copy(k):
        p = peer_tm(k)
        return pltpu.make_async_remote_copy(
            src_ref=mats_ref.at[lax.rem(p, blocks)],
            dst_ref=whole.at[t],
            send_sem=whole_s.at[k],
            recv_sem=whole_r.at[t],
            device_id={"tm": p, "grp": g},
            device_id_type=MESH,
        )

    def whole_arrival(k):
        p = peer_tm(k)
        return pltpu.make_async_remote_copy(
            src_ref=mats_ref.at[lax.rem(p, blocks)],
            dst_ref=whole.at[p],
            send_sem=whole_s.at[k],
            recv_sem=whole_r.at[p],
            device_id={"tm": p, "grp": g},
            device_id_type=MESH,
        )

    lax.fori_loop(1, count, lambda k, c: (whole_copy(k).start(), c)[1], 0)
    whole[t] = mats_ref[lax.rem(t, blocks)]
    near[groups + g] = normal_ref[...]

    @pl.when(jnp.logical_not(has_before))
    def _():
        near[0:groups] = jnp.zeros((groups, NORMAL_ROWS, LANES), F32)

    @pl.when(jnp.logical_not(has_after))
    def _():
        near[2 * groups :] = jnp.zeros((groups, NORMAL_ROWS, LANES), F32)

    each_near(lambda offset, k: near_arrival(offset, k).wait_recv())
    sums = []
    for s in range(3):
        part = near[s * groups]
        for q in range(1, groups):
            part = part + near[s * groups + q]
        sums.append(part)
    lane = lax.broadcasted_iota(jnp.int32, (NORMAL_ROWS, LANES), 1)
    before = pltpu.roll(sums[0], (HALO - nodes_dev) % LANES, 1)
    own = pltpu.roll(sums[1], HALO, 1)
    after = pltpu.roll(sums[2], (HALO + nodes_dev) % LANES, 1)
    end = nodes_dev + HALO
    normals = (
        own
        + jnp.where((lane >= 3) & (lane < HALO + 3), before, 0.0)
        + jnp.where((lane >= end) & (lane < end + HALO), after, 0.0)
    )
    spot = lax.broadcasted_iota(jnp.int32, (1, LANES), 1)
    exists = (spot >= jnp.where(has_before, 0, HALO)) & (
        spot < jnp.where(has_after, LANES, end)
    )
    normals = jnp.where(exists, normals, 0.0)
    index = {}
    for position, (a, b) in enumerate(pairs_of(3)):
        index[a, b] = index[b, a] = position
    band = [[normals[d * 6 + p : d * 6 + p + 1, :] for p in range(6)] for d in range(4)]
    right = [normals[24 + c : 25 + c, :] for c in range(3)]
    lower, inverse = cholesky_lists(symmetric(band[0], 3), 3)

    def precondition(vector):
        return solve_upper(lower, inverse, solve_lower(lower, inverse, vector))

    x = [OMEGA * value for value in precondition(right)]
    for _ in range(1, ATT_SWEEPS):
        out = [right[c] - x[c] for c in range(3)]
        for d in range(4):
            ahead = [pltpu.roll(x[c], LANES - d, 1) for c in range(3)] if d else x
            for a in range(3):
                for b in range(3):
                    out[a] = out[a] - band[d][index[a, b]] * ahead[b]
        for d in range(1, 4):
            for a in range(3):
                term = band[d][index[a, 0]] * x[0]
                for b in range(1, 3):
                    term = term + band[d][index[a, b]] * x[b]
                out[a] = out[a] - pltpu.roll(term, d, 1)
        change = precondition(out)
        x = [jnp.where(exists, x[c] + OMEGA * change[c], 0.0) for c in range(3)]
    for c in range(3):
        scaled = lower[c][c] * x[c]
        for k in range(c + 1, 3):
            scaled = scaled + lower[k][c] * x[k]
        moved = pltpu.roll(scaled, LANES - HALO, 1)
        step_ref[c : c + 1, :] = moved[:, 0:nodes_dev]


    local = kn_ref[...] - base + HALO
    tables = [jnp.broadcast_to(x[c], (tiles, LANES)) for c in range(3)]
    second = first
    for i in range(4):
        moved = ap_ref[0] * lane_pick(tables[0], local + i)
        for c in range(1, 3):
            moved = moved + ap_ref[c] * lane_pick(tables[c], local + i)
        second = second - basis[i] * moved
    second_ref[...] = second
    weighted = weights * second
    for a in range(CPAR):
        rcal[a * tiles : (a + 1) * tiles, :] = weighted * cp_ref[a]
    rcal[CPAR * tiles :, :] = jnp.zeros(((8 - CPAR) * tiles, LANES), F32)
    sums = [jnp.sum(weighted * gp_ref[a], axis=0, keepdims=True) for a in range(GPAR)]
    acc_rhs[...] = jnp.zeros_like(acc_rhs)

    def bin_rhs(no, carry):
        tile = no * 2
        units = two_rows(ci_ref, tile)
        upper, lower = lax.shift_right_logical(units, 8), lax.bitwise_and(units, 255)
        pieces = [by_high(p, upper) for p in split_three(two_tiles(rcal, tile, 8, tiles))]
        lhs = jnp.concatenate(pieces, axis=0).astype(BF16)
        acc_rhs[...] = acc_rhs[...] + dot_nt(lhs, one_hot(lower, LOW))
        return carry

    lax.fori_loop(0, tiles // 2, bin_rhs, 0, unroll=6)
    rows = 8 * (UNITS // LOW)
    total = acc_rhs[0:rows, :] + acc_rhs[rows : 2 * rows, :] + acc_rhs[2 * rows : 3 * rows, :]
    lane = lax.broadcasted_iota(jnp.int32, (1, LANES), 1)
    folded = [row + pltpu.roll(row, LANES // 2, 1) for row in sums]
    packed = [jnp.where(lane < LANES // 2, folded[2 * k], folded[2 * k + 1]) for k in range(2)]
    if rhs_ref.shape[2] > LANES:
        rhs_ref[...] = jnp.zeros_like(rhs_ref)
    for block, at, h, start in block_pieces(blocks):
        rhs_ref[block, 0:CPAR, at : at + LANES] = total[
            h * 8 : h * 8 + CPAR, start : start + LANES
        ]
        if at == 0:
            for k in range(2):
                rhs_ref[block, CPAR + k : CPAR + k + 1, 0:LANES] = packed[k]

    width = rhs_ref.shape[2]
    block = lax.rem(t, blocks)
    family = t - block

    def rwhole_copy(k, slot):
        p = peer_tm(k)
        return pltpu.make_async_remote_copy(
            src_ref=rhs_ref.at[lax.rem(p, blocks)],
            dst_ref=rwhole.at[slot],
            send_sem=rwhole_s.at[k],
            recv_sem=rwhole_r.at[slot],
            device_id={"tm": p, "grp": g},
            device_id_type=MESH,
        )

    lax.fori_loop(1, count, lambda k, c: (rwhole_copy(k, t).start(), c)[1], 0)
    rwhole[t] = rhs_ref[block]
    lax.fori_loop(1, count, lambda k, c: (whole_arrival(k).wait_recv(), c)[1], 0)
    mine[g] = lax.fori_loop(1, count, lambda k, c: c + whole[k], whole[0])

    def mine_copy(k):
        return pltpu.make_async_remote_copy(
            src_ref=mine.at[g],
            dst_ref=mine.at[g],
            send_sem=mine_s.at[k],
            recv_sem=mine_r.at[g],
            device_id={"tm": t, "grp": peer_grp(k)},
            device_id_type=MESH,
        )

    def mine_arrival(k):
        q = peer_grp(k)
        return pltpu.make_async_remote_copy(
            src_ref=mine.at[q],
            dst_ref=mine.at[q],
            send_sem=mine_s.at[k],
            recv_sem=mine_r.at[q],
            device_id={"tm": t, "grp": q},
            device_id_type=MESH,
        )

    for k in range(1, groups):
        mine_copy(k).start()
    for k in range(1, groups):
        mine_arrival(k).wait_recv()
    total = mine[0]
    for q in range(1, groups):
        total = total + mine[q]
    unit_total = total
    matrix = [unit_total[p : p + 1, :] for p in range(21)]
    lower, inverse = cholesky_lists(symmetric(matrix, CPAR), CPAR)
    upper_g = [
        jnp.broadcast_to(
            jnp.sum(unit_total[21 + p : 22 + p, 0:LANES], axis=1, keepdims=True), (1, LANES)
        )
        for p in range(10)
    ]
    lower_g, inverse_g = cholesky_lists(symmetric(upper_g, GPAR), GPAR)
    lax.fori_loop(1, count, lambda k, c: (rwhole_copy(k, peer_tm(k)).wait_recv(), c)[1], 0)
    rmine[g] = lax.fori_loop(1, count, lambda k, c: c + rwhole[k], rwhole[0])

    def rmine_copy(k, slot):
        return pltpu.make_async_remote_copy(
            src_ref=rmine.at[slot],
            dst_ref=rmine.at[slot],
            send_sem=rmine_s.at[k],
            recv_sem=rmine_r.at[slot],
            device_id={"tm": t, "grp": peer_grp(k)},
            device_id_type=MESH,
        )

    for k in range(1, groups):
        rmine_copy(k, g).start()
    for k in range(1, groups):
        rmine_copy(k, peer_grp(k)).wait_recv()
    total = rmine[0]
    for q in range(1, groups):
        total = total + rmine[q]
    right = [total[c : c + 1, :] for c in range(CPAR)]
    white = solve_lower(lower, inverse, right)
    solved = solve_upper(lower, inverse, white)
    for c in range(CPAR):
        ready[c : c + 1, :] = white[c]
        ready[CPAR + c : CPAR + c + 1, :] = solved[c]
    ready[2 * CPAR :, :] = jnp.zeros((16 - 2 * CPAR, width), F32)

    def spread_copy(k, slot):
        return pltpu.make_async_remote_copy(
            src_ref=ready,
            dst_ref=spread.at[slot],
            send_sem=spread_s.at[k],
            recv_sem=spread_r.at[slot],
            device_id={"tm": family + lax.rem(block + k, blocks), "grp": g},
            device_id_type=MESH,
        )

    lax.fori_loop(1, blocks, lambda k, c: (spread_copy(k, block).start(), c)[1], 0)
    spread[block] = ready[...]
    lane = lax.broadcasted_iota(jnp.int32, (1, LANES), 1)
    right_g = []
    for c in range(GPAR):
        row = total[CPAR + c // 2 : CPAR + c // 2 + 1, 0:LANES]
        half = (lane < LANES // 2) if c % 2 == 0 else (lane >= LANES // 2)
        value = jnp.sum(jnp.where(half, row, 0.0), axis=1, keepdims=True)
        right_g.append(jnp.broadcast_to(value, (1, LANES)))
    white_g = solve_lower(lower_g, inverse_g, right_g)
    solved_g = solve_upper(lower_g, inverse_g, white_g)
    for c in range(GPAR):
        glob_ref[c : c + 1, :] = white_g[c]
        glob_ref[GPAR + c : GPAR + c + 1, :] = solved_g[c]
    lax.fori_loop(
        1,
        blocks,
        lambda k, c: (spread_copy(k, lax.rem(block + k, blocks)).wait_recv(), c)[1],
        0,
    )
    out_ref[...] = spread[...]
    lax.fori_loop(1, count, lambda k, c: (rwhole_copy(k, t).wait_send(), c)[1], 0)
    for k in range(1, groups):
        rmine_copy(k, g).wait_send()
    lax.fori_loop(1, blocks, lambda k, c: (spread_copy(k, block).wait_send(), c)[1], 0)
    for k in range(1, groups):
        mine_copy(k).wait_send()
    each_near(lambda offset, k: near_copy(offset, k).wait_send())
    lax.fori_loop(1, count, lambda k, c: (whole_copy(k).wait_send(), c)[1], 0)


def final_kernel(
    blocks, second_ref, solved_ref, glob_ref, att_ref, cp_ref, ci_ref, gp_ref,
    res_ref, att_out_ref, step_ref, glob_out_ref,
):
    att_out_ref[...] = att_ref[...]
    lane = lax.broadcasted_iota(jnp.int32, (1, LANES), 1)
    packed = jnp.zeros((1, LANES), F32)
    for c in range(GPAR):
        packed = jnp.where(lane == c, glob_ref[c : c + 1, :], packed)
    glob_out_ref[...] = packed[:, 0:GPAR]
    tiles = second_ref.shape[0]
    units = ci_ref[...]
    high, low = lax.shift_right_logical(units, 7), lax.bitwise_and(units, 127)
    picked = [jnp.zeros((tiles, LANES), F32) for _ in range(CPAR)]
    width = UNITS // blocks
    for row in range(UNITS // LANES):
        block, at = (row * LANES) // width, (row * LANES) % width
        here = high == row
        step_ref[:, row * LANES : (row + 1) * LANES] = solved_ref[block, 0:CPAR, at : at + LANES]
        for c in range(CPAR):
            line = solved_ref[block, CPAR + c : CPAR + c + 1, at : at + LANES]
            table = jnp.broadcast_to(line, (tiles, LANES))
            picked[c] = jnp.where(here, lane_pick(table, low), picked[c])
    out = second_ref[...]
    for c in range(CPAR):
        out = out - cp_ref[c] * picked[c]
    for c in range(GPAR):
        out = out - gp_ref[c] * glob_ref[GPAR + c : GPAR + c + 1, :]
    res_ref[...] = out


def per_device(
    shape, residual, weight, source_part, source_index, source_delta, attitude_part,
    spline_phase, knot_index, calib_part, calib_index, global_part,
):
    count, groups, blocks = shape
    row_count = residual.shape[-1]
    tiles = row_count // TILE
    nodes_dev = tiles * KPT
    width = UNITS // blocks

    def flat(value):
        return value.reshape(tiles, TILE)

    def deep(value):
        return value.reshape(value.shape[0], -1, LANES)

    weights, phase, knots, units = map(flat, (weight, spline_phase, knot_index, calib_index))
    axes, calib, glob = map(deep, (attitude_part, calib_part, global_part))

    def out(*dims):
        return jax.ShapeDtypeStruct(dims, F32)

    dma = pltpu.SemaphoreType.DMA
    second, attitude_step, solved, global_out = pl.pallas_call(
        functools.partial(step_kernel, shape, nodes_dev),
        out_shape=(
            out(tiles, LANES), out(3, nodes_dev), out(blocks, 16, width), out(2 * GPAR, LANES),
        ),
        scratch_shapes=[
            pltpu.VMEM((ATT_ROWS * tiles, LANES), F32),
            pltpu.VMEM((UNIT_ROWS * tiles, LANES), F32),
            pltpu.VMEM((8 * tiles, LANES), F32),
            pltpu.VMEM((ATT_ROWS, LANES), F32),
            pltpu.VMEM((UNIT_ROWS * (UNITS // LOW), LOW), F32),
            pltpu.VMEM((3 * 8 * (UNITS // LOW), LOW), F32),
            pltpu.VMEM((NORMAL_ROWS, LANES), F32),
            pltpu.VMEM((blocks, NORMAL_ROWS, width), F32),
            pltpu.VMEM((blocks, 8, width), F32),
            pltpu.VMEM((3 * groups, NORMAL_ROWS, LANES), F32),
            pltpu.VMEM((groups, NORMAL_ROWS, width), F32),
            pltpu.VMEM((count, NORMAL_ROWS, width), F32),
            pltpu.VMEM((count, 8, width), F32),
            pltpu.VMEM((groups, 8, width), F32),
            pltpu.VMEM((16, width), F32),
            pltpu.VMEM((blocks, 16, width), F32),
            dma((3 * groups,)), dma((3 * groups,)),
            dma((groups,)), dma((groups,)),
            dma((count,)), dma((count,)),
            dma((count,)), dma((count,)),
            dma((groups,)), dma((groups,)),
            dma((blocks,)), dma((blocks,)),
        ],
        in_specs=[pl.BlockSpec(memory_space=pltpu.VMEM)] * 11,
        compiler_params=pltpu.CompilerParams(collective_id=0, has_side_effects=True),
        name="step",
    )(
        flat(residual), weights, deep(source_part), flat(source_index), deep(source_delta),
        axes, phase, knots, calib, units, glob,
    )
    final, attitude_out, calib_step, global_step = pl.pallas_call(
        functools.partial(final_kernel, blocks),
        out_shape=(
            out(tiles, LANES), out(3, nodes_dev), out(CPAR, UNITS), out(1, GPAR),
        ),
        name="final",
    )(second, solved, global_out, attitude_step, calib, units, glob)
    return final.reshape(residual.shape), attitude_out, calib_step, global_step.reshape(GPAR)


def solution(mesh):
    count, groups = mesh.shape["tm"], mesh.shape["grp"]
    blocks = min(count, UNITS // LANES)
    return jax.shard_map(
        functools.partial(per_device, (count, groups, blocks)),
        mesh=mesh,
        in_specs=(
            P("tm", "grp", None),
            P("tm", "grp", None),
            P(None, "tm", "grp", None),
            P("tm", "grp", None),
            P(None, "tm", None),
            P(None, "tm", "grp", None),
            P("tm", "grp", None),
            P("tm", "grp", None),
            P(None, "tm", "grp", None),
            P("tm", "grp", None),
            P(None, "tm", "grp", None),
        ),
        out_specs=(P("tm", "grp", None), P(None, "tm"), P(), P()),
        check_vma=False,
    )
```

profile of v0, /device:TPU:0, one launch (start us, length us, event | category | flops | bytes accessed | tf_op | source)
XLA Modules:
  0.0 32.9 jit_solution(2459827685905155834)
XLA Ops:
  0.6 29.9 %step.1 = (f32[24,128]{1,0:T(8,128)}, f32[3,96]{1,0:T(4,128)}, f32[16,16,128]{2,1,0:T(8,128)}, f32[8,128]{1,0:T(8,128)}) custom-call(f32[24,128]{1,0:T(8,128)} %bitcast.22, f32[24,128]{1,0:T(8,128)} %bitcast.23, f32[5,24,128]{2,1,0:T(8,128)} %bitcast.18, s32[24,128]{1,0:T(8,128)} %bitcast.24, f32[5,32,128]{2,1,0:T(8,128)} %bitcast.17, ...), custom_call_target="tpu_custom_call" | custom-call | tf_op jit(solution)/shard_map/step/pallas_call | solution.py:626
  30.5 2.4 %final.1 = (f32[24,128]{1,0:T(8,128)}, f32[3,96]{1,0:T(4,128)}, f32[6,2048]{1,0:T(8,128)}, f32[1,4]{1,0:T(1,128)}) custom-call(f32[24,128]{1,0:T(8,128)} %get-tuple-element.12.second_ref, f32[16,16,128]{2,1,0:T(8,128)} %get-tuple-element.13.solved_ref, f32[8,128]{1,0:T(8,128)} %get-tuple-element.14.glob_ref, f32[3,96]{1,0:T(4,128)} %get-tuple-element.15.att_ref, ...), custom_call_target="tpu_custom_call" | custom-call | tf_op jit(solution)/shard_map/final/pallas_call | solution.py:662
where the time goes:
time: 33.1 us; the launch traced here: 32.9 us
  Pallas kernels  32.3 us (98%)
  between operations  0.64 us (2%)
    pallas_call x1, Pallas kernels, per_device(): pl.pallas_call(functools.partial(step_kernel, shape, nodes_dev), out_shap...  29.9 us
    pallas_call x1, Pallas kernels, per_device(): pl.pallas_call(functools.partial(final_kernel, blocks), out_shape=(out(ti...  2.4 us

commit v1 on v0

v1 whole, which is shorter than its diff:
```python
import functools
import math

import jax
import jax.numpy as jnp
from jax import lax
from jax.experimental import pallas as pl
from jax.experimental.pallas import tpu as pltpu
from jax.sharding import PartitionSpec as P

TILE = 128
KPT = 4
UNITS = 2048
CPAR = 6
GPAR = 4
ATT_SWEEPS = 4

OMEGA = 0.6
RIDGE = 1.0
LANES = 128
LOW = 256
HALO = 3 * ATT_SWEEPS
MESH = pl.DeviceIdType.MESH
F32 = jnp.float32
BF16 = jnp.bfloat16

ATT_ROWS = 72
UNIT_ROWS = 24
PAIRS = CPAR * (CPAR + 1) // 2
HALF = 64
NORMAL_ROWS = 32


def pairs_of(extent):
    return [(a, b) for a in range(extent) for b in range(a, extent)]


def lane_pick(table, index):
    return lax.gather(
        table,
        index[..., None],
        lax.GatherDimensionNumbers(
            offset_dims=(),
            collapsed_slice_dims=(1,),
            start_index_map=(1,),
            operand_batching_dims=(0,),
            start_indices_batching_dims=(0,),
        ),
        (1, 1),
        mode=lax.GatherScatterMode.PROMISE_IN_BOUNDS,
    )


def spline_basis(phase):
    inverse = 1.0 - phase
    square = phase * phase
    cubed = square * phase
    return [
        inverse * inverse * inverse / 6.0,
        (3.0 * cubed - 6.0 * square + 4.0) / 6.0,
        (-3.0 * cubed + 3.0 * square + 3.0 * phase + 1.0) / 6.0,
        cubed / 6.0,
    ]


def cholesky_lists(matrix, extent):
    lower = [[None] * extent for _ in range(extent)]
    inverse = [None] * extent
    for column in range(extent):
        pivot = matrix[column][column]
        for k in range(column):
            pivot = pivot - lower[column][k] * lower[column][k]
        root = jnp.sqrt(pivot)
        lower[column][column] = root
        inverse[column] = 1.0 / root
        for row in range(column + 1, extent):
            entry = matrix[row][column]
            for k in range(column):
                entry = entry - lower[row][k] * lower[column][k]
            lower[row][column] = entry * inverse[column]
    return lower, inverse


def solve_lower(lower, inverse, vector):
    result = []
    for row in range(len(vector)):
        running = vector[row]
        for k in range(row):
            running = running - lower[row][k] * result[k]
        result.append(running * inverse[row])
    return result


def solve_upper(lower, inverse, vector):
    extent = len(vector)
    result = [None] * extent
    for row in reversed(range(extent)):
        running = vector[row]
        for k in range(row + 1, extent):
            running = running - lower[k][row] * result[k]
        result[row] = running * inverse[row]
    return result


def symmetric(upper, extent):
    matrix = [[None] * extent for _ in range(extent)]
    for position, (a, b) in enumerate(pairs_of(extent)):
        value = upper[position] + (RIDGE if a == b else 0.0)
        matrix[a][b] = value
        matrix[b][a] = value
    return matrix


def split_two(value):
    first = value.astype(BF16)
    return [first, (value - first.astype(F32)).astype(BF16)]


def dot_nt(left, right):
    return lax.dot_general(
        left, right, (((1,), (1,)), ((), ())), preferred_element_type=F32
    )


def two_tiles(ref, tile, rows, tiles):
    return jnp.concatenate(
        [ref[pl.ds(tile, rows, stride=tiles), :], ref[pl.ds(tile + 1, rows, stride=tiles), :]],
        axis=1,
    )


def two_rows(ref, tile):
    return jnp.concatenate([ref[pl.ds(tile, 1), :], ref[pl.ds(tile + 1, 1), :]], axis=1)


def one_hot(row, extent):
    spots = lax.broadcasted_iota(jnp.int32, (extent, row.shape[1]), 0)
    return jnp.where(spots == row, 1.0, 0.0).astype(BF16)


def by_high(part, high):
    return jnp.concatenate(
        [jnp.where(high == h, part, 0.0) for h in range(UNITS // LOW)], axis=0
    ).astype(BF16)


def block_pieces(blocks):
    width = UNITS // blocks
    for piece in range(UNITS // LANES):
        unit = piece * LANES
        yield unit // width, unit % width, unit // LOW, unit % LOW


def round_up(value, unit):
    return -(-value // unit) * unit


def layout(shape):
    count, groups, inner = shape
    plane = groups * inner
    blocks = min(plane, UNITS // LANES)
    width = UNITS // blocks
    slots = width // HALF
    mats_rows = round_up(PAIRS + -(-(GPAR * (GPAR + 1) // 2) // slots), 8)
    rhs_rows = round_up(CPAR + -(-GPAR // slots), 8)
    parts = width // LANES
    ready_rows = round_up(2 * CPAR * parts, 8)
    return plane, blocks, width, slots, mats_rows, rhs_rows, parts, ready_rows


def solved_rows(parts, ready_rows):
    spare = [8 * j + r for j in range(parts) for r in range(CPAR, 8)]
    return spare + list(range(8 * parts, ready_rows))


def fold_slots(rows, slots):
    lane = lax.broadcasted_iota(jnp.int32, (1, LANES), 1)
    folded = [row + pltpu.roll(row, HALF, 1) for row in rows]
    folded.append(jnp.zeros((1, LANES), F32))
    packed = []
    for start in range(0, len(rows), slots):
        parts = []
        for k in range(start, start + slots, 2):
            left, right = folded[min(k, len(rows))], folded[min(k + 1, len(rows))]
            parts.append(jnp.where(lane < HALF, left, right))
        packed.append(parts)
    return packed


def slot_sum(table, first_row, no, slots):
    row, at = first_row + no // slots, no % slots
    start = (at // 2) * LANES
    lane = lax.broadcasted_iota(jnp.int32, (1, LANES), 1)
    half = (lane < HALF) if at % 2 == 0 else (lane >= HALF)
    values = jnp.where(half, table[row : row + 1, start : start + LANES], 0.0)
    return jnp.broadcast_to(jnp.sum(values, axis=1, keepdims=True), (1, LANES))


def step_kernel(
    shape, nodes_dev,
    res_h, w_h, sp_h, si_h, sd_h, ap_h, ph_h, kn_h, cp_h, ci_h, gp_h,
    out_ref, step_ref, cstep_ref, glob_ref,
    res_ref, w_ref, sp_ref, si_ref, sd_ref, ap_ref, ph_ref, kn_ref, cp_ref, ci_ref, gp_ref,
    att, cal, rcal, acc_att, acc_cal, acc_rhs, normal_ref, mats_ref, rhs_ref,
    near, pmat, prhs, zmat, zrhs, ready, spread,
    load_s, near_s, near_r, pmat_s, pmat_r, prhs_s, prhs_r,
    zmat_s, zmat_r, zrhs_s, zrhs_r, spread_s, spread_r,
):
    count, groups, inner = shape
    plane, blocks, width, slots, mats_rows, rhs_rows, parts, ready_rows = layout(shape)
    depth = count // inner
    t, g = lax.axis_index("tm"), lax.axis_index("grp")
    has_before, has_after = t > 0, t < count - 1
    z, i = lax.div(t, inner), lax.rem(t, inner)
    m = g * inner + i
    block = lax.rem(m, blocks)
    family = m - block

    pairs = [
        (si_h, si_ref), (sd_h, sd_ref), (sp_h, sp_ref), (res_h, res_ref), (w_h, w_ref),
        (ap_h, ap_ref), (ph_h, ph_ref), (kn_h, kn_ref), (cp_h, cp_ref), (ci_h, ci_ref),
        (gp_h, gp_ref),
    ]
    loads = [
        pltpu.make_async_copy(source, target, load_s.at[no])
        for no, (source, target) in enumerate(pairs)
    ]
    for load in loads:
        load.start()

    def peer_tm(k):
        return lax.rem(t + k, count)

    def peer_grp(k):
        return lax.rem(g + k, groups)

    def member(p):
        return {"tm": z * inner + lax.rem(p, inner), "grp": lax.div(p, inner)}

    def level(k):
        return {"tm": lax.rem(t + k * inner, count), "grp": g}

    barrier = pltpu.get_barrier_semaphore()

    def greet(where):
        pl.semaphore_signal(barrier, inc=1, device_id=where, device_id_type=MESH)

    for k in range(1, depth):
        greet(level(k))
    for k in range(groups):
        greet({"tm": peer_tm(1), "grp": peer_grp(k)})
        greet({"tm": peer_tm(count - 1), "grp": peer_grp(k)})
    for k in range(1, plane):
        greet(member(lax.rem(m + k, plane)))

    for load in loads[:8]:
        load.wait()
    tiles = res_ref.shape[0]
    weights = w_ref[...]
    sources = si_ref[...]
    high, low = lax.shift_right_logical(sources, 7), lax.bitwise_and(sources, 127)
    picked = [jnp.zeros((tiles, LANES), F32) for _ in range(5)]
    for row in range(sd_ref.shape[1]):
        here = high == row
        for c in range(5):
            table = jnp.broadcast_to(sd_ref[c, row : row + 1, :], (tiles, LANES))
            picked[c] = jnp.where(here, lane_pick(table, low), picked[c])
    total = sp_ref[0] * picked[0]
    for c in range(1, 5):
        total = total + sp_ref[c] * picked[c]
    first = res_ref[...] - total
    basis = spline_basis(ph_ref[...])
    axes = [ap_ref[c] for c in range(3)]
    products = [weights * axes[a] * axes[b] for a, b in pairs_of(3)]
    rights = [weights * axes[a] * first for a in range(3)]
    place = 0
    for i_ in range(4):
        for d in range(4 - i_):
            both = basis[i_] * basis[i_ + d]
            for product in products:
                att[place * tiles : (place + 1) * tiles, :] = both * product
                place += 1
    for i_ in range(4):
        for right in rights:
            att[place * tiles : (place + 1) * tiles, :] = basis[i_] * right
            place += 1
    acc_att[...] = jnp.zeros_like(acc_att)
    base = t * (tiles * KPT)

    def bin_nodes(no, carry):
        tile = no * 2
        knots = two_rows(kn_ref, tile) - base
        nodes = one_hot(knots, LANES)
        part = acc_att[...]
        for piece in split_two(two_tiles(att, tile, ATT_ROWS, tiles)):
            part = part + dot_nt(piece, nodes)
        acc_att[...] = part
        return carry

    lax.fori_loop(0, tiles // 2, bin_nodes, 0, unroll=6)
    band = [None] * 5
    place = 0
    for i_ in range(4):
        for d in list(range(4 - i_)):
            rows = acc_att[place : place + 6, :]
            rows = pltpu.roll(rows, i_, 1) if i_ else rows
            band[d] = rows if band[d] is None else band[d] + rows
            place += 6
    for i_ in range(4):
        rows = acc_att[place : place + 3, :]
        rows = pltpu.roll(rows, i_, 1) if i_ else rows
        band[4] = rows if band[4] is None else band[4] + rows
        place += 3
    for d in range(4):
        normal_ref[d * 6 : (d + 1) * 6, :] = band[d]
    normal_ref[24:27, :] = band[4]
    normal_ref[27:, :] = jnp.zeros((NORMAL_ROWS - 27, LANES), F32)
    pl.semaphore_wait(barrier, depth - 1 + 2 * groups + plane - 1)

    def near_copy(offset, k):
        slot = (1 - offset) * groups + g
        return pltpu.make_async_remote_copy(
            src_ref=normal_ref,
            dst_ref=near.at[slot],
            send_sem=near_s.at[(offset + 1) * groups + k],
            recv_sem=near_r.at[slot],
            device_id={"tm": t + offset, "grp": peer_grp(k)},
            device_id_type=MESH,
        )

    def near_arrival(offset, k):
        slot = (offset + 1) * groups + peer_grp(k)
        return pltpu.make_async_remote_copy(
            src_ref=normal_ref,
            dst_ref=near.at[slot],
            send_sem=near_s.at[(offset + 1) * groups + k],
            recv_sem=near_r.at[slot],
            device_id={"tm": t + offset, "grp": peer_grp(k)},
            device_id_type=MESH,
        )

    def each_near(do):
        @pl.when(has_before)
        def _():
            for k in reversed(range(groups)):
                do(-1, k)

        @pl.when(has_after)
        def _():
            for k in reversed(range(groups)):
                do(1, k)

        for k in range(1, groups):
            do(0, k)

    each_near(lambda offset, k: near_copy(offset, k).start())

    for load in loads[8:]:
        load.wait()
    place = 0
    for a, b in pairs_of(CPAR):
        cal[place * tiles : (place + 1) * tiles, :] = weights * cp_ref[a] * cp_ref[b]
        place += 1
    cal[place * tiles :, :] = jnp.zeros(((UNIT_ROWS - place) * tiles, LANES), F32)
    global_rows = fold_slots(
        [
            jnp.sum(weights * gp_ref[a] * gp_ref[b], axis=0, keepdims=True)
            for a, b in pairs_of(GPAR)
        ],
        slots,
    )
    acc_cal[...] = jnp.zeros_like(acc_cal)

    def bin_units(no, carry):
        tile = no * 2
        units = two_rows(ci_ref, tile)
        upper, lower = lax.shift_right_logical(units, 8), lax.bitwise_and(units, 255)
        spots = one_hot(lower, LOW)
        part = acc_cal[...]
        for piece in split_two(two_tiles(cal, tile, UNIT_ROWS, tiles)):
            part = part + dot_nt(by_high(piece.astype(F32), upper), spots)
        acc_cal[...] = part
        return carry

    lax.fori_loop(0, tiles // 2, bin_units, 0, unroll=6)
    for b_, at, h, start in block_pieces(blocks):
        mats_ref[b_, 0:UNIT_ROWS, at : at + LANES] = acc_cal[
            h * UNIT_ROWS : (h + 1) * UNIT_ROWS, start : start + LANES
        ]
    if mats_rows > UNIT_ROWS:
        mats_ref[:, UNIT_ROWS:, :] = jnp.zeros((blocks, mats_rows - UNIT_ROWS, width), F32)
    for b_ in range(blocks):
        for no, pieces in enumerate(global_rows):
            for j, piece in enumerate(pieces):
                mats_ref[b_, PAIRS + no : PAIRS + no + 1, j * LANES : (j + 1) * LANES] = piece

    def plane_copy(source, target, send, recv, k, slot):
        p = lax.rem(m + k, plane)
        return pltpu.make_async_remote_copy(
            src_ref=source.at[lax.rem(p, blocks)],
            dst_ref=target.at[slot],
            send_sem=send.at[k],
            recv_sem=recv.at[slot],
            device_id=member(p),
            device_id_type=MESH,
        )

    def level_copy(target, send, recv, k, slot):
        return pltpu.make_async_remote_copy(
            src_ref=target.at[slot],
            dst_ref=target.at[slot],
            send_sem=send.at[k],
            recv_sem=recv.at[slot],
            device_id=level(k),
            device_id_type=MESH,
        )

    def slots_total(buffer, number):
        out = buffer[0]
        for k in range(1, number):
            out = out + buffer[k]
        return out

    for k in range(1, plane):
        plane_copy(mats_ref, pmat, pmat_s, pmat_r, k, m).start()
    pmat[m] = mats_ref[block]
    near[groups + g] = normal_ref[...]

    @pl.when(jnp.logical_not(has_before))
    def _():
        near[0:groups] = jnp.zeros((groups, NORMAL_ROWS, LANES), F32)

    @pl.when(jnp.logical_not(has_after))
    def _():
        near[2 * groups :] = jnp.zeros((groups, NORMAL_ROWS, LANES), F32)

    each_near(lambda offset, k: near_arrival(offset, k).wait_recv())
    sums = []
    for s in range(3):
        part = near[s * groups]
        for q in range(1, groups):
            part = part + near[s * groups + q]
        sums.append(part)
    lane = lax.broadcasted_iota(jnp.int32, (NORMAL_ROWS, LANES), 1)
    before = pltpu.roll(sums[0], (HALO - nodes_dev) % LANES, 1)
    own = pltpu.roll(sums[1], HALO, 1)
    after = pltpu.roll(sums[2], (HALO + nodes_dev) % LANES, 1)
    end = nodes_dev + HALO
    normals = (
        own
        + jnp.where((lane >= 3) & (lane < HALO + 3), before, 0.0)
        + jnp.where((lane >= end) & (lane < end + HALO), after, 0.0)
    )
    spot = lax.broadcasted_iota(jnp.int32, (1, LANES), 1)
    exists = (spot >= jnp.where(has_before, 0, HALO)) & (
        spot < jnp.where(has_after, LANES, end)
    )
    normals = jnp.where(exists, normals, 0.0)
    index = {}
    for position, (a, b) in enumerate(pairs_of(3)):
        index[a, b] = index[b, a] = position
    band = [[normals[d * 6 + p : d * 6 + p + 1, :] for p in range(6)] for d in range(4)]
    right = [normals[24 + c : 25 + c, :] for c in range(3)]
    lower, inverse = cholesky_lists(symmetric(band[0], 3), 3)

    def precondition(vector):
        return solve_upper(lower, inverse, solve_lower(lower, inverse, vector))

    x = [OMEGA * value for value in precondition(right)]
    for _ in range(1, ATT_SWEEPS):
        out = [right[c] - x[c] for c in range(3)]
        for d in range(4):
            ahead = [pltpu.roll(x[c], LANES - d, 1) for c in range(3)] if d else x
            for a in range(3):
                for b in range(3):
                    out[a] = out[a] - band[d][index[a, b]] * ahead[b]
        for d in range(1, 4):
            for a in range(3):
                term = band[d][index[a, 0]] * x[0]
                for b in range(1, 3):
                    term = term + band[d][index[a, b]] * x[b]
                out[a] = out[a] - pltpu.roll(term, d, 1)
        change = precondition(out)
        x = [jnp.where(exists, x[c] + OMEGA * change[c], 0.0) for c in range(3)]

    local = kn_ref[...] - base + HALO
    tables = [jnp.broadcast_to(x[c], (tiles, LANES)) for c in range(3)]
    second = first
    for i_ in range(4):
        moved = ap_ref[0] * lane_pick(tables[0], local + i_)
        for c in range(1, 3):
            moved = moved + ap_ref[c] * lane_pick(tables[c], local + i_)
        second = second - basis[i_] * moved
    out_ref[...] = second
    weighted = weights * second
    for a in range(CPAR):
        rcal[a * tiles : (a + 1) * tiles, :] = weighted * cp_ref[a]
    rcal[CPAR * tiles :, :] = jnp.zeros(((8 - CPAR) * tiles, LANES), F32)
    global_rows = fold_slots(
        [jnp.sum(weighted * gp_ref[a], axis=0, keepdims=True) for a in range(GPAR)], slots
    )
    acc_rhs[...] = jnp.zeros_like(acc_rhs)

    def bin_rhs(no, carry):
        tile = no * 2
        units = two_rows(ci_ref, tile)
        upper, lower = lax.shift_right_logical(units, 8), lax.bitwise_and(units, 255)
        pieces = [
            by_high(p.astype(F32), upper) for p in split_two(two_tiles(rcal, tile, 8, tiles))
        ]
        lhs = jnp.concatenate(pieces, axis=0)
        acc_rhs[...] = acc_rhs[...] + dot_nt(lhs, one_hot(lower, LOW))
        return carry

    lax.fori_loop(0, tiles // 2, bin_rhs, 0, unroll=6)
    rows = 8 * (UNITS // LOW)
    total = acc_rhs[0:rows, :] + acc_rhs[rows : 2 * rows, :]
    for b_, at, h, start in block_pieces(blocks):
        rhs_ref[b_, 0:8, at : at + LANES] = total[h * 8 : h * 8 + 8, start : start + LANES]
    for b_ in range(blocks):
        for no, pieces in enumerate(global_rows):
            for j, piece in enumerate(pieces):
                rhs_ref[b_, CPAR + no : CPAR + no + 1, j * LANES : (j + 1) * LANES] = piece
    for k in range(1, plane):
        plane_copy(rhs_ref, prhs, prhs_s, prhs_r, k, m).start()
    prhs[m] = rhs_ref[block]

    for c in range(3):
        scaled = lower[c][c] * x[c]
        for k in range(c + 1, 3):
            scaled = scaled + lower[k][c] * x[k]
        moved = pltpu.roll(scaled, LANES - HALO, 1)
        step_ref[c : c + 1, :] = moved[:, 0:nodes_dev]

    for k in range(1, plane):
        plane_copy(mats_ref, pmat, pmat_s, pmat_r, k, lax.rem(m + k, plane)).wait_recv()
    zmat[z] = slots_total(pmat, plane)
    for k in range(1, depth):
        level_copy(zmat, zmat_s, zmat_r, k, z).start()

    for k in range(1, plane):
        plane_copy(rhs_ref, prhs, prhs_s, prhs_r, k, lax.rem(m + k, plane)).wait_recv()
    zrhs[z] = slots_total(prhs, plane)
    for k in range(1, depth):
        level_copy(zrhs, zrhs_s, zrhs_r, k, z).start()

    for k in range(1, depth):
        level_copy(zmat, zmat_s, zmat_r, k, lax.rem(z + k, depth)).wait_recv()
    unit_total = slots_total(zmat, depth)
    matrix = [unit_total[p : p + 1, :] for p in range(PAIRS)]
    lower, inverse = cholesky_lists(symmetric(matrix, CPAR), CPAR)
    upper_g = [
        slot_sum(unit_total, PAIRS, p, slots) for p in range(GPAR * (GPAR + 1) // 2)
    ]
    lower_g, inverse_g = cholesky_lists(symmetric(upper_g, GPAR), GPAR)

    for k in range(1, depth):
        level_copy(zrhs, zrhs_s, zrhs_r, k, lax.rem(z + k, depth)).wait_recv()
    total = slots_total(zrhs, depth)
    right = [total[c : c + 1, :] for c in range(CPAR)]
    white = solve_lower(lower, inverse, right)
    solved = solve_upper(lower, inverse, white)
    where_solved = solved_rows(parts, ready_rows)
    for j in range(parts):
        span = slice(j * LANES, (j + 1) * LANES)
        for c in range(CPAR):
            ready[8 * j + c : 8 * j + c + 1, :] = white[c][:, span]
            row = where_solved[c * parts + j]
            ready[row : row + 1, :] = solved[c][:, span]
    for row in where_solved[CPAR * parts :]:
        ready[row : row + 1, :] = jnp.zeros((1, LANES), F32)

    def spread_copy(k, slot):
        return pltpu.make_async_remote_copy(
            src_ref=ready,
            dst_ref=spread.at[slot],
            send_sem=spread_s.at[k],
            recv_sem=spread_r.at[slot],
            device_id=member(family + lax.rem(block + k, blocks)),
            device_id_type=MESH,
        )

    for k in range(1, blocks):
        spread_copy(k, block).start()
    spread[block] = ready[...]
    right_g = [slot_sum(total, CPAR, c, slots) for c in range(GPAR)]
    white_g = solve_lower(lower_g, inverse_g, right_g)
    solved_g = solve_upper(lower_g, inverse_g, white_g)
    spot = lax.broadcasted_iota(jnp.int32, (1, LANES), 1)
    packed = jnp.zeros((1, LANES), F32)
    for c in range(GPAR):
        packed = jnp.where(spot == c, white_g[c], packed)
    glob_ref[...] = packed[:, 0:GPAR]
    out = out_ref[...]
    for c in range(GPAR):
        out = out - gp_ref[c] * solved_g[c]
    units = ci_ref[...]
    high, low = lax.shift_right_logical(units, 7), lax.bitwise_and(units, 127)
    for k in range(1, blocks):
        spread_copy(k, lax.rem(block + k, blocks)).wait_recv()
    picked = [jnp.zeros((tiles, LANES), F32) for _ in range(CPAR)]
    for b_ in range(blocks):
        for j in range(parts):
            row = b_ * parts + j
            here = high == row
            cstep_ref[:, row * LANES : (row + 1) * LANES] = spread[b_, 8 * j : 8 * j + CPAR, :]
            for c in range(CPAR):
                at = where_solved[c * parts + j]
                table = jnp.broadcast_to(spread[b_, at : at + 1, :], (tiles, LANES))
                picked[c] = jnp.where(here, lane_pick(table, low), picked[c])
    for c in range(CPAR):
        out = out - cp_ref[c] * picked[c]
    out_ref[...] = out
    each_near(lambda offset, k: near_copy(offset, k).wait_send())
    for k in range(1, plane):
        plane_copy(mats_ref, pmat, pmat_s, pmat_r, k, m).wait_send()
        plane_copy(rhs_ref, prhs, prhs_s, prhs_r, k, m).wait_send()
    for k in range(1, depth):
        level_copy(zmat, zmat_s, zmat_r, k, z).wait_send()
        level_copy(zrhs, zrhs_s, zrhs_r, k, z).wait_send()
    for k in range(1, blocks):
        spread_copy(k, block).wait_send()


def final_kernel(*refs):
    half = len(refs) // 2
    copies = [
        pltpu.make_async_copy(refs[no], refs[half + no], refs[-1].at[no]) for no in range(half)
    ]
    for copy in copies:
        copy.start()
    for copy in copies:
        copy.wait()


def per_device(
    shape, residual, weight, source_part, source_index, source_delta, attitude_part,
    spline_phase, knot_index, calib_part, calib_index, global_part,
):
    count, groups, inner = shape
    plane, blocks, width, slots, mats_rows, rhs_rows, parts, ready_rows = layout(shape)
    depth = count // inner
    row_count = residual.shape[-1]
    tiles = row_count // TILE
    nodes_dev = tiles * KPT

    def flat(value):
        return value.reshape(tiles, TILE)

    def deep(value):
        return value.reshape(value.shape[0], -1, LANES)

    args = (
        flat(residual), flat(weight), deep(source_part), flat(source_index),
        deep(source_delta), deep(attitude_part), flat(spline_phase), flat(knot_index),
        deep(calib_part), flat(calib_index), deep(global_part),
    )

    def vmem(*dims):
        return pltpu.VMEM(dims, F32)

    dma = pltpu.SemaphoreType.DMA
    results = pl.pallas_call(
        functools.partial(step_kernel, shape, nodes_dev),
        out_shape=(
            vmem(tiles, LANES), vmem(3, nodes_dev), vmem(CPAR, UNITS), vmem(1, GPAR),
        ),
        scratch_shapes=[pltpu.VMEM(arg.shape, arg.dtype) for arg in args] + [
            vmem(ATT_ROWS * tiles, LANES),
            vmem(UNIT_ROWS * tiles, LANES),
            vmem(8 * tiles, LANES),
            vmem(ATT_ROWS, LANES),
            vmem(UNIT_ROWS * (UNITS // LOW), LOW),
            vmem(2 * 8 * (UNITS // LOW), LOW),
            vmem(NORMAL_ROWS, LANES),
            vmem(blocks, mats_rows, width),
            vmem(blocks, rhs_rows, width),
            vmem(3 * groups, NORMAL_ROWS, LANES),
            vmem(plane, mats_rows, width),
            vmem(plane, rhs_rows, width),
            vmem(depth, mats_rows, width),
            vmem(depth, rhs_rows, width),
            vmem(ready_rows, LANES),
            vmem(blocks, ready_rows, LANES),
            dma((len(args),)),
            dma((3 * groups,)), dma((3 * groups,)),
            dma((plane,)), dma((plane,)),
            dma((plane,)), dma((plane,)),
            dma((depth,)), dma((depth,)),
            dma((depth,)), dma((depth,)),
            dma((blocks,)), dma((blocks,)),
        ],
        in_specs=[pl.BlockSpec(memory_space=pl.ANY)] * len(args),
        compiler_params=pltpu.CompilerParams(collective_id=0, has_side_effects=True),
        name="step",
    )(*args)
    final, attitude_out, calib_step, global_step = pl.pallas_call(
        final_kernel,
        out_shape=tuple(jax.ShapeDtypeStruct(value.shape, F32) for value in results),
        in_specs=[pl.BlockSpec(memory_space=pltpu.VMEM)] * len(results),
        out_specs=(pl.BlockSpec(memory_space=pltpu.HBM),) * len(results),
        scratch_shapes=[dma((len(results),))],
        name="final",
    )(*[pltpu.with_memory_space_constraint(value, pltpu.VMEM) for value in results])
    return final.reshape(residual.shape), attitude_out, calib_step, global_step.reshape(GPAR)


def solution(mesh):
    count, groups = mesh.shape["tm"], mesh.shape["grp"]
    inner = 1 << (int(math.log2(count)) // 2)
    return jax.shard_map(
        functools.partial(per_device, (count, groups, inner)),
        mesh=mesh,
        in_specs=(
            P("tm", "grp", None),
            P("tm", "grp", None),
            P(None, "tm", "grp", None),
            P("tm", "grp", None),
            P(None, "tm", None),
            P(None, "tm", "grp", None),
            P("tm", "grp", None),
            P("tm", "grp", None),
            P(None, "tm", "grp", None),
            P("tm", "grp", None),
            P(None, "tm", "grp", None),
        ),
        out_specs=(P("tm", "grp", None), P(None, "tm"), P(), P()),
        check_vma=False,
    )
```

time: 33.1 us -> 24.8 us (0.75)
  Pallas kernels: 32.3 us -> 23.9 us
    pallas_call x1, Pallas kernels: 29.9 us -> 23.2 us  [per_device(): pl.pallas_call(functools.partial(step_kernel, shape, nodes_dev), out_shap...]
    pallas_call x1, Pallas kernels: 2.4 us -> 0.68 us  [per_device(): pl.pallas_call(final_kernel, out_shape=tuple((jax.ShapeDtypeStruct(value....]
where the time goes in v1:
time: 24.8 us; the launch traced here: 24.5 us
  Pallas kernels  23.9 us (96%)
  between operations  0.64 us (3%)
    pallas_call x1, Pallas kernels, per_device(): pl.pallas_call(functools.partial(step_kernel, shape, nodes_dev), out_shap...  23.2 us
    pallas_call x1, Pallas kernels, per_device(): pl.pallas_call(final_kernel, out_shape=tuple((jax.ShapeDtypeStruct(value....  0.68 us

profile of v1, /device:TPU:0, one launch (start us, length us, event | category | flops | bytes accessed | tf_op | source)
XLA Modules:
  0.0 24.5 jit_solution(2433971391612864109)
XLA Ops:
  0.6 23.2 %step.1 = (f32[24,128]{1,0:T(8,128)S(1)}, f32[3,96]{1,0:T(4,128)S(1)}, f32[6,2048]{1,0:T(8,128)S(1)}, f32[1,4]{1,0:T(1,128)S(1)}) custom-call(f32[24,128]{1,0:T(8,128)} %bitcast.18, f32[24,128]{1,0:T(8,128)} %bitcast.19, f32[5,24,128]{2,1,0:T(8,128)} %bitcast.15, s32[24,128]{1,0:T(8,128)} %bitcast.20, f32[5,32,128]{2,1,0:T(8,128)} %bitcast.13, ...), custom_call_target="tpu_custom_call" | custom-call | tf_op jit(solution)/shard_map/step/pallas_call | solution.py:663
  23.9 0.7 %final.1 = (f32[24,128]{1,0:T(8,128)}, f32[3,96]{1,0:T(4,128)}, f32[6,2048]{1,0:T(8,128)}, f32[1,4]{1,0:T(1,128)}) custom-call(f32[24,128]{1,0:T(8,128)S(1)} %get-tuple-element.12.refs_0_, f32[3,96]{1,0:T(4,128)S(1)} %get-tuple-element.13.refs_1_, f32[6,2048]{1,0:T(8,128)S(1)} %get-tuple-element.14.refs_2_, f32[1,4]{1,0:T(1,128)S(1)} %get-tuple-element.15.refs_3_), custom_call_target="tpu_custom_call" | custom-call | tf_op jit(solution)/shard_map/final/pallas_call | solution.py:697

commit v2 on v1

--- a/solution.py
+++ b/solution.py
@@ -164,13 +164,18 @@
     mats_rows = round_up(PAIRS + -(-(GPAR * (GPAR + 1) // 2) // slots), 8)
     rhs_rows = round_up(CPAR + -(-GPAR // slots), 8)
     parts = width // LANES
-    ready_rows = round_up(2 * CPAR * parts, 8)
-    return plane, blocks, width, slots, mats_rows, rhs_rows, parts, ready_rows
-
-
-def solved_rows(parts, ready_rows):
-    spare = [8 * j + r for j in range(parts) for r in range(CPAR, 8)]
-    return spare + list(range(8 * parts, ready_rows))
+    return plane, blocks, width, slots, mats_rows, rhs_rows, parts
+
+
+def partner(place, k, size):
+    if size & (size - 1):
+        return lax.rem(place + k, size)
+    other, bit = place, 1
+    while bit < size:
+        if k & bit:
+            other = other + bit - 2 * bit * lax.rem(lax.div(place, bit), 2)
+        bit *= 2
+    return other
 
 
 def fold_slots(rows, slots):
@@ -201,13 +206,14 @@
     res_h, w_h, sp_h, si_h, sd_h, ap_h, ph_h, kn_h, cp_h, ci_h, gp_h,
     out_ref, step_ref, cstep_ref, glob_ref,
     res_ref, w_ref, sp_ref, si_ref, sd_ref, ap_ref, ph_ref, kn_ref, cp_ref, ci_ref, gp_ref,
-    att, cal, rcal, acc_att, acc_cal, acc_rhs, normal_ref, mats_ref, rhs_ref,
-    near, pmat, prhs, zmat, zrhs, ready, spread,
+    first_ref, att, att_two, node_spots, unit_spots, cal, rcal, acc_att, acc_cal,
+    normal_ref, mats_ref, rhs_ref,
+    near, pmat, prhs, zmat, zrhs, solved_ref, solved_all, white_ref, white_all,
     load_s, near_s, near_r, pmat_s, pmat_r, prhs_s, prhs_r,
-    zmat_s, zmat_r, zrhs_s, zrhs_r, spread_s, spread_r,
+    zmat_s, zmat_r, zrhs_s, zrhs_r, solved_s, solved_r, white_s, white_r,
 ):
     count, groups, inner = shape
-    plane, blocks, width, slots, mats_rows, rhs_rows, parts, ready_rows = layout(shape)
+    plane, blocks, width, slots, mats_rows, rhs_rows, parts = layout(shape)
     depth = count // inner
     t, g = lax.axis_index("tm"), lax.axis_index("grp")
     has_before, has_after = t > 0, t < count - 1
@@ -251,24 +257,37 @@
         greet({"tm": peer_tm(1), "grp": peer_grp(k)})
         greet({"tm": peer_tm(count - 1), "grp": peer_grp(k)})
     for k in range(1, plane):
-        greet(member(lax.rem(m + k, plane)))
-
-    for load in loads[:8]:
+        greet(member(partner(m, k, plane)))
+
+    for load in loads[:4]:
         load.wait()
     tiles = res_ref.shape[0]
+    source_rows = sd_ref.shape[1]
+    table = jnp.concatenate(
+        split_two(sd_ref[...].reshape(5 * source_rows, LANES)), axis=1
+    )
+    for tile in range(0, tiles, 2):
+        sources = two_rows(si_ref, tile)
+        high, low = lax.shift_right_logical(sources, 7), lax.bitwise_and(sources, 127)
+        spots = one_hot(low, LANES)
+        found = jnp.dot(
+            table, jnp.concatenate([spots, spots], axis=0), preferred_element_type=F32
+        )
+        total = None
+        for c in range(5):
+            factor = jnp.concatenate(
+                [sp_ref[c, tile : tile + 1, :], sp_ref[c, tile + 1 : tile + 2, :]], axis=1
+            )
+            term = found[c * source_rows : (c + 1) * source_rows, :] * factor
+            total = term if total is None else total + term
+        levels = lax.broadcasted_iota(jnp.int32, (source_rows, 2 * LANES), 0)
+        total = jnp.sum(jnp.where(levels == high, total, 0.0), axis=0, keepdims=True)
+        first_ref[tile : tile + 1, :] = res_ref[tile : tile + 1, :] - total[:, :LANES]
+        first_ref[tile + 1 : tile + 2, :] = res_ref[tile + 1 : tile + 2, :] - total[:, LANES:]
+    for load in loads[4:8]:
+        load.wait()
     weights = w_ref[...]
-    sources = si_ref[...]
-    high, low = lax.shift_right_logical(sources, 7), lax.bitwise_and(sources, 127)
-    picked = [jnp.zeros((tiles, LANES), F32) for _ in range(5)]
-    for row in range(sd_ref.shape[1]):
-        here = high == row
-        for c in range(5):
-            table = jnp.broadcast_to(sd_ref[c, row : row + 1, :], (tiles, LANES))
-            picked[c] = jnp.where(here, lane_pick(table, low), picked[c])
-    total = sp_ref[0] * picked[0]
-    for c in range(1, 5):
-        total = total + sp_ref[c] * picked[c]
-    first = res_ref[...] - total
+    first = first_ref[...]
     basis = spline_basis(ph_ref[...])
     axes = [ap_ref[c] for c in range(3)]
     products = [weights * axes[a] * axes[b] for a, b in pairs_of(3)]
@@ -284,20 +303,14 @@
         for right in rights:
             att[place * tiles : (place + 1) * tiles, :] = basis[i_] * right
             place += 1
-    acc_att[...] = jnp.zeros_like(acc_att)
     base = t * (tiles * KPT)
-
-    def bin_nodes(no, carry):
-        tile = no * 2
-        knots = two_rows(kn_ref, tile) - base
-        nodes = one_hot(knots, LANES)
-        part = acc_att[...]
-        for piece in split_two(two_tiles(att, tile, ATT_ROWS, tiles)):
-            part = part + dot_nt(piece, nodes)
-        acc_att[...] = part
-        return carry
-
-    lax.fori_loop(0, tiles // 2, bin_nodes, 0, unroll=6)
+    for tile in range(tiles):
+        span = slice(tile * LANES, (tile + 1) * LANES)
+        value = att[pl.ds(tile, ATT_ROWS, stride=tiles), :]
+        att_two[:, span] = jnp.concatenate(split_two(value), axis=0)
+        node_spots[:, span] = one_hot(kn_ref[tile : tile + 1, :] - base, LANES)
+    sums = dot_nt(att_two[...], node_spots[...])
+    acc_att[...] = sums[:ATT_ROWS] + sums[ATT_ROWS:]
     band = [None] * 5
     place = 0
     for i_ in range(4):
@@ -376,6 +389,7 @@
         units = two_rows(ci_ref, tile)
         upper, lower = lax.shift_right_logical(units, 8), lax.bitwise_and(units, 255)
         spots = one_hot(lower, LOW)
+        unit_spots[no] = spots
         part = acc_cal[...]
         for piece in split_two(two_tiles(cal, tile, UNIT_ROWS, tiles)):
             part = part + dot_nt(by_high(piece.astype(F32), upper), spots)
@@ -395,7 +409,7 @@
                 mats_ref[b_, PAIRS + no : PAIRS + no + 1, j * LANES : (j + 1) * LANES] = piece
 
     def plane_copy(source, target, send, recv, k, slot):
-        p = lax.rem(m + k, plane)
+        p = partner(m, k, plane)
         return pltpu.make_async_remote_copy(
             src_ref=source.at[lax.rem(p, blocks)],
             dst_ref=target.at[slot],
@@ -421,7 +435,7 @@
             out = out + buffer[k]
         return out
 
-    for k in range(1, plane):
+    for k in reversed(range(1, plane)):
         plane_copy(mats_ref, pmat, pmat_s, pmat_r, k, m).start()
     pmat[m] = mats_ref[block]
     near[groups + g] = normal_ref[...]
@@ -499,29 +513,24 @@
     global_rows = fold_slots(
         [jnp.sum(weighted * gp_ref[a], axis=0, keepdims=True) for a in range(GPAR)], slots
     )
-    acc_rhs[...] = jnp.zeros_like(acc_rhs)
-
-    def bin_rhs(no, carry):
+    acc = None
+    for no in range(tiles // 2):
         tile = no * 2
-        units = two_rows(ci_ref, tile)
-        upper, lower = lax.shift_right_logical(units, 8), lax.bitwise_and(units, 255)
+        upper = lax.shift_right_logical(two_rows(ci_ref, tile), 8)
         pieces = [
             by_high(p.astype(F32), upper) for p in split_two(two_tiles(rcal, tile, 8, tiles))
         ]
-        lhs = jnp.concatenate(pieces, axis=0)
-        acc_rhs[...] = acc_rhs[...] + dot_nt(lhs, one_hot(lower, LOW))
-        return carry
-
-    lax.fori_loop(0, tiles // 2, bin_rhs, 0, unroll=6)
+        part = dot_nt(jnp.concatenate(pieces, axis=0), unit_spots[no])
+        acc = part if acc is None else acc + part
     rows = 8 * (UNITS // LOW)
-    total = acc_rhs[0:rows, :] + acc_rhs[rows : 2 * rows, :]
+    total = acc[0:rows, :] + acc[rows : 2 * rows, :]
     for b_, at, h, start in block_pieces(blocks):
         rhs_ref[b_, 0:8, at : at + LANES] = total[h * 8 : h * 8 + 8, start : start + LANES]
     for b_ in range(blocks):
         for no, pieces in enumerate(global_rows):
             for j, piece in enumerate(pieces):
                 rhs_ref[b_, CPAR + no : CPAR + no + 1, j * LANES : (j + 1) * LANES] = piece
-    for k in range(1, plane):
+    for k in reversed(range(1, plane)):
         plane_copy(rhs_ref, prhs, prhs_s, prhs_r, k, m).start()
     prhs[m] = rhs_ref[block]
 
@@ -533,13 +542,13 @@
         step_ref[c : c + 1, :] = moved[:, 0:nodes_dev]
 
     for k in range(1, plane):
-        plane_copy(mats_ref, pmat, pmat_s, pmat_r, k, lax.rem(m + k, plane)).wait_recv()
+        plane_copy(mats_ref, pmat, pmat_s, pmat_r, k, partner(m, k, plane)).wait_recv()
     zmat[z] = slots_total(pmat, plane)
     for k in range(1, depth):
         level_copy(zmat, zmat_s, zmat_r, k, z).start()
 
     for k in range(1, plane):
-        plane_copy(rhs_ref, prhs, prhs_s, prhs_r, k, lax.rem(m + k, plane)).wait_recv()
+        plane_copy(rhs_ref, prhs, prhs_s, prhs_r, k, partner(m, k, plane)).wait_recv()
     zrhs[z] = slots_total(prhs, plane)
     for k in range(1, depth):
         level_copy(zrhs, zrhs_s, zrhs_r, k, z).start()
@@ -560,29 +569,29 @@
     right = [total[c : c + 1, :] for c in range(CPAR)]
     white = solve_lower(lower, inverse, right)
     solved = solve_upper(lower, inverse, white)
-    where_solved = solved_rows(parts, ready_rows)
-    for j in range(parts):
-        span = slice(j * LANES, (j + 1) * LANES)
-        for c in range(CPAR):
-            ready[8 * j + c : 8 * j + c + 1, :] = white[c][:, span]
-            row = where_solved[c * parts + j]
-            ready[row : row + 1, :] = solved[c][:, span]
-    for row in where_solved[CPAR * parts :]:
-        ready[row : row + 1, :] = jnp.zeros((1, LANES), F32)
-
-    def spread_copy(k, slot):
+    for c in range(CPAR):
+        for j in range(parts):
+            row = c * parts + j
+            solved_ref[row : row + 1, :] = solved[c][:, j * LANES : (j + 1) * LANES]
+
+    def spread_copy(source, target, send, recv, k, slot):
         return pltpu.make_async_remote_copy(
-            src_ref=ready,
-            dst_ref=spread.at[slot],
-            send_sem=spread_s.at[k],
-            recv_sem=spread_r.at[slot],
-            device_id=member(family + lax.rem(block + k, blocks)),
+            src_ref=source,
+            dst_ref=target.at[slot],
+            send_sem=send.at[k],
+            recv_sem=recv.at[slot],
+            device_id=member(family + partner(block, k, blocks)),
             device_id_type=MESH,
         )
 
-    for k in range(1, blocks):
-        spread_copy(k, block).start()
-    spread[block] = ready[...]
+    for k in reversed(range(1, blocks)):
+        spread_copy(solved_ref, solved_all, solved_s, solved_r, k, block).start()
+    for c in range(CPAR):
+        white_ref[c : c + 1, :] = white[c]
+    for k in reversed(range(1, blocks)):
+        spread_copy(white_ref, white_all, white_s, white_r, k, block).start()
+    solved_all[block] = solved_ref[...]
+    white_all[block] = white_ref[...]
     right_g = [slot_sum(total, CPAR, c, slots) for c in range(GPAR)]
     white_g = solve_lower(lower_g, inverse_g, right_g)
     solved_g = solve_upper(lower_g, inverse_g, white_g)
@@ -596,21 +605,27 @@
         out = out - gp_ref[c] * solved_g[c]
     units = ci_ref[...]
     high, low = lax.shift_right_logical(units, 7), lax.bitwise_and(units, 127)
-    for k in range(1, blocks):
-        spread_copy(k, lax.rem(block + k, blocks)).wait_recv()
     picked = [jnp.zeros((tiles, LANES), F32) for _ in range(CPAR)]
-    for b_ in range(blocks):
+    for k in range(blocks):
+        source = partner(block, k, blocks)
+        if k:
+            spread_copy(solved_ref, solved_all, solved_s, solved_r, k, source).wait_recv()
         for j in range(parts):
-            row = b_ * parts + j
-            here = high == row
-            cstep_ref[:, row * LANES : (row + 1) * LANES] = spread[b_, 8 * j : 8 * j + CPAR, :]
+            here = high == source * parts + j
             for c in range(CPAR):
-                at = where_solved[c * parts + j]
-                table = jnp.broadcast_to(spread[b_, at : at + 1, :], (tiles, LANES))
+                row = c * parts + j
+                table = jnp.broadcast_to(
+                    solved_all[source, row : row + 1, :], (tiles, LANES)
+                )
                 picked[c] = jnp.where(here, lane_pick(table, low), picked[c])
     for c in range(CPAR):
         out = out - cp_ref[c] * picked[c]
     out_ref[...] = out
+    for k in range(1, blocks):
+        source = partner(block, k, blocks)
+        spread_copy(white_ref, white_all, white_s, white_r, k, source).wait_recv()
+    for b_ in range(blocks):
+        cstep_ref[:, b_ * width : (b_ + 1) * width] = white_all[b_]
     each_near(lambda offset, k: near_copy(offset, k).wait_send())
     for k in range(1, plane):
         plane_copy(mats_ref, pmat, pmat_s, pmat_r, k, m).wait_send()
@@ -619,7 +634,8 @@
         level_copy(zmat, zmat_s, zmat_r, k, z).wait_send()
         level_copy(zrhs, zrhs_s, zrhs_r, k, z).wait_send()
     for k in range(1, blocks):
-        spread_copy(k, block).wait_send()
+        spread_copy(solved_ref, solved_all, solved_s, solved_r, k, block).wait_send()
+        spread_copy(white_ref, white_all, white_s, white_r, k, block).wait_send()
 
 
 def final_kernel(*refs):
@@ -638,7 +654,7 @@
     spline_phase, knot_index, calib_part, calib_index, global_part,
 ):
     count, groups, inner = shape
-    plane, blocks, width, slots, mats_rows, rhs_rows, parts, ready_rows = layout(shape)
+    plane, blocks, width, slots, mats_rows, rhs_rows, parts = layout(shape)
     depth = count // inner
     row_count = residual.shape[-1]
     tiles = row_count // TILE
@@ -666,12 +682,15 @@
             vmem(tiles, LANES), vmem(3, nodes_dev), vmem(CPAR, UNITS), vmem(1, GPAR),
         ),
         scratch_shapes=[pltpu.VMEM(arg.shape, arg.dtype) for arg in args] + [
+            vmem(tiles, LANES),
             vmem(ATT_ROWS * tiles, LANES),
+            pltpu.VMEM((2 * ATT_ROWS, row_count), BF16),
+            pltpu.VMEM((LANES, row_count), BF16),
+            pltpu.VMEM((tiles // 2, LOW, 2 * LANES), BF16),
             vmem(UNIT_ROWS * tiles, LANES),
             vmem(8 * tiles, LANES),
             vmem(ATT_ROWS, LANES),
             vmem(UNIT_ROWS * (UNITS // LOW), LOW),
-            vmem(2 * 8 * (UNITS // LOW), LOW),
             vmem(NORMAL_ROWS, LANES),
             vmem(blocks, mats_rows, width),
             vmem(blocks, rhs_rows, width),
@@ -680,14 +699,17 @@
             vmem(plane, rhs_rows, width),
             vmem(depth, mats_rows, width),
             vmem(depth, rhs_rows, width),
-            vmem(ready_rows, LANES),
-            vmem(blocks, ready_rows, LANES),
+            vmem(CPAR * parts, LANES),
+            vmem(blocks, CPAR * parts, LANES),
+            vmem(CPAR, width),
+            vmem(blocks, CPAR, width),
             dma((len(args),)),
             dma((3 * groups,)), dma((3 * groups,)),
             dma((plane,)), dma((plane,)),
             dma((plane,)), dma((plane,)),
             dma((depth,)), dma((depth,)),
             dma((depth,)), dma((depth,)),
+            dma((blocks,)), dma((blocks,)),
             dma((blocks,)), dma((blocks,)),
         ],
         in_specs=[pl.BlockSpec(memory_space=pl.ANY)] * len(args),

time: 24.8 us -> 23.5 us (0.948)
  Pallas kernels: 23.9 us -> 22.6 us
    pallas_call x1, Pallas kernels: 23.2 us -> 21.9 us  [per_device(): pl.pallas_call(functools.partial(step_kernel, shape, nodes_dev), out_shap...]
where the time goes in v2:
time: 23.5 us; the launch traced here: 23.2 us
  Pallas kernels  22.6 us (96%)
  between operations  0.64 us (3%)
    pallas_call x1, Pallas kernels, per_device(): pl.pallas_call(functools.partial(step_kernel, shape, nodes_dev), out_shap...  21.9 us
    pallas_call x1, Pallas kernels, per_device(): pl.pallas_call(final_kernel, out_shape=tuple((jax.ShapeDtypeStruct(value....  0.68 us

profile of v2, /device:TPU:0, one launch (start us, length us, event | category | flops | bytes accessed | tf_op | source)
XLA Modules:
  0.0 23.2 jit_solution(18156711938513279312)
XLA Ops:
  0.6 21.9 %step.1 = (f32[24,128]{1,0:T(8,128)S(1)}, f32[3,96]{1,0:T(4,128)S(1)}, f32[6,2048]{1,0:T(8,128)S(1)}, f32[1,4]{1,0:T(1,128)S(1)}) custom-call(f32[24,128]{1,0:T(8,128)} %bitcast.18, f32[24,128]{1,0:T(8,128)} %bitcast.19, f32[5,24,128]{2,1,0:T(8,128)} %bitcast.15, s32[24,128]{1,0:T(8,128)} %bitcast.20, f32[5,32,128]{2,1,0:T(8,128)} %bitcast.13, ...), custom_call_target="tpu_custom_call" | custom-call | tf_op jit(solution)/shard_map/step/pallas_call | solution.py:679
  22.5 0.7 %final.1 = (f32[24,128]{1,0:T(8,128)}, f32[3,96]{1,0:T(4,128)}, f32[6,2048]{1,0:T(8,128)}, f32[1,4]{1,0:T(1,128)}) custom-call(f32[24,128]{1,0:T(8,128)S(1)} %get-tuple-element.12.refs_0_, f32[3,96]{1,0:T(4,128)S(1)} %get-tuple-element.13.refs_1_, f32[6,2048]{1,0:T(8,128)S(1)} %get-tuple-element.14.refs_2_, f32[1,4]{1,0:T(1,128)S(1)} %get-tuple-element.15.refs_3_), custom_call_target="tpu_custom_call" | custom-call | tf_op jit(solution)/shard_map/final/pallas_call | solution.py:719

commit v3 on v2

--- a/solution.py
+++ b/solution.py
@@ -158,7 +158,7 @@
 def layout(shape):
     count, groups, inner = shape
     plane = groups * inner
-    blocks = min(plane, UNITS // LANES)
+    blocks = plane // 2
     width = UNITS // blocks
     slots = width // HALF
     mats_rows = round_up(PAIRS + -(-(GPAR * (GPAR + 1) // 2) // slots), 8)
@@ -219,23 +219,30 @@
     has_before, has_after = t > 0, t < count - 1
     z, i = lax.div(t, inner), lax.rem(t, inner)
     m = g * inner + i
-    block = lax.rem(m, blocks)
-    family = m - block
+    block = lax.div(m, 2)
+    owner = lax.rem(m, 2) == 1
+    follower = jnp.logical_not(owner)
 
     pairs = [
         (si_h, si_ref), (sd_h, sd_ref), (sp_h, sp_ref), (res_h, res_ref), (w_h, w_ref),
         (ap_h, ap_ref), (ph_h, ph_ref), (kn_h, kn_ref), (cp_h, cp_ref), (ci_h, ci_ref),
         (gp_h, gp_ref),
     ]
+    stages = [pairs[:4], pairs[4:8], pairs[8:]]
     loads = [
         pltpu.make_async_copy(source, target, load_s.at[no])
-        for no, (source, target) in enumerate(pairs)
+        for no, stage in enumerate(stages)
+        for source, target in stage
     ]
     for load in loads:
         load.start()
 
-    def peer_tm(k):
-        return lax.rem(t + k, count)
+    def drain(ref, sem):
+        pltpu.make_async_copy(ref, ref, sem).wait()
+
+    def loaded(no):
+        size = sum(math.prod(target.shape) for _, target in stages[no]) // LANES
+        drain(att.at[0:size], load_s.at[no])
 
     def peer_grp(k):
         return lax.rem(g + k, groups)
@@ -253,14 +260,21 @@
 
     for k in range(1, depth):
         greet(level(k))
-    for k in range(groups):
-        greet({"tm": peer_tm(1), "grp": peer_grp(k)})
-        greet({"tm": peer_tm(count - 1), "grp": peer_grp(k)})
+
+    @pl.when(has_before)
+    def _():
+        for k in range(groups):
+            greet({"tm": t - 1, "grp": peer_grp(k)})
+
+    @pl.when(has_after)
+    def _():
+        for k in range(groups):
+            greet({"tm": t + 1, "grp": peer_grp(k)})
+
     for k in range(1, plane):
         greet(member(partner(m, k, plane)))
 
-    for load in loads[:4]:
-        load.wait()
+    loaded(0)
     tiles = res_ref.shape[0]
     source_rows = sd_ref.shape[1]
     table = jnp.concatenate(
@@ -284,8 +298,7 @@
         total = jnp.sum(jnp.where(levels == high, total, 0.0), axis=0, keepdims=True)
         first_ref[tile : tile + 1, :] = res_ref[tile : tile + 1, :] - total[:, :LANES]
         first_ref[tile + 1 : tile + 2, :] = res_ref[tile + 1 : tile + 2, :] - total[:, LANES:]
-    for load in loads[4:8]:
-        load.wait()
+    loaded(1)
     weights = w_ref[...]
     first = first_ref[...]
     basis = spline_basis(ph_ref[...])
@@ -328,26 +341,16 @@
         normal_ref[d * 6 : (d + 1) * 6, :] = band[d]
     normal_ref[24:27, :] = band[4]
     normal_ref[27:, :] = jnp.zeros((NORMAL_ROWS - 27, LANES), F32)
-    pl.semaphore_wait(barrier, depth - 1 + 2 * groups + plane - 1)
+    sides = has_before.astype(jnp.int32) + has_after.astype(jnp.int32)
+    pl.semaphore_wait(barrier, depth - 1 + plane - 1 + groups * sides)
 
     def near_copy(offset, k):
         slot = (1 - offset) * groups + g
         return pltpu.make_async_remote_copy(
             src_ref=normal_ref,
             dst_ref=near.at[slot],
-            send_sem=near_s.at[(offset + 1) * groups + k],
-            recv_sem=near_r.at[slot],
-            device_id={"tm": t + offset, "grp": peer_grp(k)},
-            device_id_type=MESH,
-        )
-
-    def near_arrival(offset, k):
-        slot = (offset + 1) * groups + peer_grp(k)
-        return pltpu.make_async_remote_copy(
-            src_ref=normal_ref,
-            dst_ref=near.at[slot],
-            send_sem=near_s.at[(offset + 1) * groups + k],
-            recv_sem=near_r.at[slot],
+            send_sem=near_s.at[offset + 1],
+            recv_sem=near_r.at[1 - offset],
             device_id={"tm": t + offset, "grp": peer_grp(k)},
             device_id_type=MESH,
         )
@@ -366,10 +369,21 @@
         for k in range(1, groups):
             do(0, k)
 
+    def drain_near(sems):
+        @pl.when(has_before)
+        def _():
+            drain(near.at[0:groups], sems.at[0])
+
+        @pl.when(has_after)
+        def _():
+            drain(near.at[0:groups], sems.at[2])
+
+        if groups > 1:
+            drain(near.at[0 : groups - 1], sems.at[1])
+
     each_near(lambda offset, k: near_copy(offset, k).start())
 
-    for load in loads[8:]:
-        load.wait()
+    loaded(2)
     place = 0
     for a, b in pairs_of(CPAR):
         cal[place * tiles : (place + 1) * tiles, :] = weights * cp_ref[a] * cp_ref[b]
@@ -408,26 +422,46 @@
             for j, piece in enumerate(pieces):
                 mats_ref[b_, PAIRS + no : PAIRS + no + 1, j * LANES : (j + 1) * LANES] = piece
 
-    def plane_copy(source, target, send, recv, k, slot):
-        p = partner(m, k, plane)
-        return pltpu.make_async_remote_copy(
-            src_ref=source.at[lax.rem(p, blocks)],
-            dst_ref=target.at[slot],
-            send_sem=send.at[k],
-            recv_sem=recv.at[slot],
-            device_id=member(p),
-            device_id_type=MESH,
-        )
-
-    def level_copy(target, send, recv, k, slot):
-        return pltpu.make_async_remote_copy(
-            src_ref=target.at[slot],
-            dst_ref=target.at[slot],
-            send_sem=send.at[k],
-            recv_sem=recv.at[slot],
-            device_id=level(k),
-            device_id_type=MESH,
-        )
+    def to_owners(source, target, send, recv):
+        def copy(k):
+            p = partner(block, k, blocks)
+            pltpu.make_async_remote_copy(
+                src_ref=source.at[p],
+                dst_ref=target.at[m],
+                send_sem=send.at[min(k, 1)],
+                recv_sem=recv.at[0],
+                device_id=member(2 * p + 1),
+                device_id_type=MESH,
+            ).start()
+
+        for k in reversed(range(1, blocks)):
+            copy(k)
+
+        @pl.when(follower)
+        def _():
+            copy(0)
+
+        @pl.when(owner)
+        def _():
+            target[m] = source[block]
+
+    def sent_to_owners(source, send):
+        drain(source.at[0 : blocks - 1], send.at[1])
+
+        @pl.when(follower)
+        def _():
+            drain(source.at[0:1], send.at[0])
+
+    def to_levels(target, send, recv):
+        for k in range(1, depth):
+            pltpu.make_async_remote_copy(
+                src_ref=target.at[z],
+                dst_ref=target.at[z],
+                send_sem=send.at[0],
+                recv_sem=recv.at[0],
+                device_id=level(k),
+                device_id_type=MESH,
+            ).start()
 
     def slots_total(buffer, number):
         out = buffer[0]
@@ -435,9 +469,7 @@
             out = out + buffer[k]
         return out
 
-    for k in reversed(range(1, plane)):
-        plane_copy(mats_ref, pmat, pmat_s, pmat_r, k, m).start()
-    pmat[m] = mats_ref[block]
+    to_owners(mats_ref, pmat, pmat_s, pmat_r)
     near[groups + g] = normal_ref[...]
 
     @pl.when(jnp.logical_not(has_before))
@@ -448,7 +480,7 @@
     def _():
         near[2 * groups :] = jnp.zeros((groups, NORMAL_ROWS, LANES), F32)
 
-    each_near(lambda offset, k: near_arrival(offset, k).wait_recv())
+    drain_near(near_r)
     sums = []
     for s in range(3):
         part = near[s * groups]
@@ -530,9 +562,7 @@
         for no, pieces in enumerate(global_rows):
             for j, piece in enumerate(pieces):
                 rhs_ref[b_, CPAR + no : CPAR + no + 1, j * LANES : (j + 1) * LANES] = piece
-    for k in reversed(range(1, plane)):
-        plane_copy(rhs_ref, prhs, prhs_s, prhs_r, k, m).start()
-    prhs[m] = rhs_ref[block]
+    to_owners(rhs_ref, prhs, prhs_s, prhs_r)
 
     for c in range(3):
         scaled = lower[c][c] * x[c]
@@ -541,75 +571,74 @@
         moved = pltpu.roll(scaled, LANES - HALO, 1)
         step_ref[c : c + 1, :] = moved[:, 0:nodes_dev]
 
-    for k in range(1, plane):
-        plane_copy(mats_ref, pmat, pmat_s, pmat_r, k, partner(m, k, plane)).wait_recv()
-    zmat[z] = slots_total(pmat, plane)
-    for k in range(1, depth):
-        level_copy(zmat, zmat_s, zmat_r, k, z).start()
-
-    for k in range(1, plane):
-        plane_copy(rhs_ref, prhs, prhs_s, prhs_r, k, partner(m, k, plane)).wait_recv()
-    zrhs[z] = slots_total(prhs, plane)
-    for k in range(1, depth):
-        level_copy(zrhs, zrhs_s, zrhs_r, k, z).start()
-
-    for k in range(1, depth):
-        level_copy(zmat, zmat_s, zmat_r, k, lax.rem(z + k, depth)).wait_recv()
-    unit_total = slots_total(zmat, depth)
-    matrix = [unit_total[p : p + 1, :] for p in range(PAIRS)]
-    lower, inverse = cholesky_lists(symmetric(matrix, CPAR), CPAR)
-    upper_g = [
-        slot_sum(unit_total, PAIRS, p, slots) for p in range(GPAR * (GPAR + 1) // 2)
-    ]
-    lower_g, inverse_g = cholesky_lists(symmetric(upper_g, GPAR), GPAR)
-
-    for k in range(1, depth):
-        level_copy(zrhs, zrhs_s, zrhs_r, k, lax.rem(z + k, depth)).wait_recv()
-    total = slots_total(zrhs, depth)
-    right = [total[c : c + 1, :] for c in range(CPAR)]
-    white = solve_lower(lower, inverse, right)
-    solved = solve_upper(lower, inverse, white)
-    for c in range(CPAR):
-        for j in range(parts):
-            row = c * parts + j
-            solved_ref[row : row + 1, :] = solved[c][:, j * LANES : (j + 1) * LANES]
-
-    def spread_copy(source, target, send, recv, k, slot):
-        return pltpu.make_async_remote_copy(
-            src_ref=source,
-            dst_ref=target.at[slot],
-            send_sem=send.at[k],
-            recv_sem=recv.at[slot],
-            device_id=member(family + partner(block, k, blocks)),
-            device_id_type=MESH,
-        )
-
-    for k in reversed(range(1, blocks)):
-        spread_copy(solved_ref, solved_all, solved_s, solved_r, k, block).start()
-    for c in range(CPAR):
-        white_ref[c : c + 1, :] = white[c]
-    for k in reversed(range(1, blocks)):
-        spread_copy(white_ref, white_all, white_s, white_r, k, block).start()
-    solved_all[block] = solved_ref[...]
-    white_all[block] = white_ref[...]
-    right_g = [slot_sum(total, CPAR, c, slots) for c in range(GPAR)]
-    white_g = solve_lower(lower_g, inverse_g, right_g)
-    solved_g = solve_upper(lower_g, inverse_g, white_g)
-    spot = lax.broadcasted_iota(jnp.int32, (1, LANES), 1)
-    packed = jnp.zeros((1, LANES), F32)
-    for c in range(GPAR):
-        packed = jnp.where(spot == c, white_g[c], packed)
-    glob_ref[...] = packed[:, 0:GPAR]
-    out = out_ref[...]
-    for c in range(GPAR):
-        out = out - gp_ref[c] * solved_g[c]
+    def spread(source, target, send, recv):
+        for p in reversed(range(1, plane)):
+            to = partner(m, p, plane)
+            pltpu.make_async_remote_copy(
+                src_ref=source,
+                dst_ref=target.at[block],
+                send_sem=send.at[0],
+                recv_sem=recv.at[p // 2],
+                device_id=member(to),
+                device_id_type=MESH,
+            ).start()
+
+    @pl.when(owner)
+    def _():
+        drain(pmat.at[0 : plane - 1], pmat_r.at[0])
+        zmat[z] = slots_total(pmat, plane)
+        to_levels(zmat, zmat_s, zmat_r)
+
+        drain(prhs.at[0 : plane - 1], prhs_r.at[0])
+        zrhs[z] = slots_total(prhs, plane)
+        to_levels(zrhs, zrhs_s, zrhs_r)
+
+        drain(zmat.at[0 : depth - 1], zmat_r.at[0])
+        unit_total = slots_total(zmat, depth)
+        matrix = [unit_total[p : p + 1, :] for p in range(PAIRS)]
+        lower, inverse = cholesky_lists(symmetric(matrix, CPAR), CPAR)
+        upper_g = [
+            slot_sum(unit_total, PAIRS, p, slots) for p in range(GPAR * (GPAR + 1) // 2)
+        ]
+        lower_g, inverse_g = cholesky_lists(symmetric(upper_g, GPAR), GPAR)
+
+        drain(zrhs.at[0 : depth - 1], zrhs_r.at[0])
+        total = slots_total(zrhs, depth)
+        right = [total[c : c + 1, :] for c in range(CPAR)]
+        white = solve_lower(lower, inverse, right)
+        solved = solve_upper(lower, inverse, white)
+        for c in range(CPAR):
+            for j in range(parts):
+                row = c * parts + j
+                solved_ref[row : row + 1, :] = solved[c][:, j * LANES : (j + 1) * LANES]
+        spread(solved_ref, solved_all, solved_s, solved_r)
+        for c in range(CPAR):
+            white_ref[c : c + 1, :] = white[c]
+        right_g = [slot_sum(total, CPAR, c, slots) for c in range(GPAR)]
+        white_g = solve_lower(lower_g, inverse_g, right_g)
+        solved_g = solve_upper(lower_g, inverse_g, white_g)
+        white_ref[CPAR:, :] = jnp.zeros((8 - CPAR, width), F32)
+        spot = lax.broadcasted_iota(jnp.int32, (1, LANES), 1)
+        packed = jnp.zeros((1, LANES), F32)
+        for c in range(GPAR):
+            packed = jnp.where(spot == c, white_g[c], packed)
+            packed = jnp.where(spot == GPAR + c, solved_g[c], packed)
+        white_ref[CPAR : CPAR + 1, 0:LANES] = packed
+        spread(white_ref, white_all, white_s, white_r)
+        solved_all[block] = solved_ref[...]
+        white_all[block] = white_ref[...]
+
     units = ci_ref[...]
     high, low = lax.shift_right_logical(units, 7), lax.bitwise_and(units, 127)
     picked = [jnp.zeros((tiles, LANES), F32) for _ in range(CPAR)]
     for k in range(blocks):
         source = partner(block, k, blocks)
         if k:
-            spread_copy(solved_ref, solved_all, solved_s, solved_r, k, source).wait_recv()
+            drain(solved_ref, solved_r.at[k])
+        else:
+            @pl.when(follower)
+            def _():
+                drain(solved_ref, solved_r.at[0])
         for j in range(parts):
             here = high == source * parts + j
             for c in range(CPAR):
@@ -618,24 +647,36 @@
                     solved_all[source, row : row + 1, :], (tiles, LANES)
                 )
                 picked[c] = jnp.where(here, lane_pick(table, low), picked[c])
+    out = out_ref[...]
     for c in range(CPAR):
         out = out - cp_ref[c] * picked[c]
+    for k in range(blocks):
+        if k:
+            drain(white_ref, white_r.at[k])
+        else:
+            @pl.when(follower)
+            def _():
+                drain(white_ref, white_r.at[0])
+    for b_ in range(blocks):
+        cstep_ref[:, b_ * width : (b_ + 1) * width] = white_all[b_, 0:CPAR, :]
+    packed = white_all[0, CPAR : CPAR + 1, 0:LANES]
+    glob_ref[...] = packed[:, 0:GPAR]
+    for c in range(GPAR):
+        value = packed[:, GPAR + c : GPAR + c + 1]
+        out = out - gp_ref[c] * jnp.broadcast_to(value, (1, LANES))
     out_ref[...] = out
-    for k in range(1, blocks):
-        source = partner(block, k, blocks)
-        spread_copy(white_ref, white_all, white_s, white_r, k, source).wait_recv()
-    for b_ in range(blocks):
-        cstep_ref[:, b_ * width : (b_ + 1) * width] = white_all[b_]
-    each_near(lambda offset, k: near_copy(offset, k).wait_send())
-    for k in range(1, plane):
-        plane_copy(mats_ref, pmat, pmat_s, pmat_r, k, m).wait_send()
-        plane_copy(rhs_ref, prhs, prhs_s, prhs_r, k, m).wait_send()
-    for k in range(1, depth):
-        level_copy(zmat, zmat_s, zmat_r, k, z).wait_send()
-        level_copy(zrhs, zrhs_s, zrhs_r, k, z).wait_send()
-    for k in range(1, blocks):
-        spread_copy(solved_ref, solved_all, solved_s, solved_r, k, block).wait_send()
-        spread_copy(white_ref, white_all, white_s, white_r, k, block).wait_send()
+    drain_near(near_s)
+    sent_to_owners(mats_ref, pmat_s)
+    sent_to_owners(rhs_ref, prhs_s)
+
+    @pl.when(owner)
+    def _():
+        drain(zmat.at[0 : depth - 1], zmat_s.at[0])
+        drain(zrhs.at[0 : depth - 1], zrhs_s.at[0])
+        size = (plane - 1) * math.prod(solved_ref.shape) // LANES
+        drain(att.at[0:size], solved_s.at[0])
+        size = (plane - 1) * math.prod(white_ref.shape) // LANES
+        drain(att.at[0:size], white_s.at[0])
 
 
 def final_kernel(*refs):
@@ -701,16 +742,16 @@
             vmem(depth, rhs_rows, width),
             vmem(CPAR * parts, LANES),
             vmem(blocks, CPAR * parts, LANES),
-            vmem(CPAR, width),
-            vmem(blocks, CPAR, width),
-            dma((len(args),)),
-            dma((3 * groups,)), dma((3 * groups,)),
-            dma((plane,)), dma((plane,)),
-            dma((plane,)), dma((plane,)),
-            dma((depth,)), dma((depth,)),
-            dma((depth,)), dma((depth,)),
-            dma((blocks,)), dma((blocks,)),
-            dma((blocks,)), dma((blocks,)),
+            vmem(8, width),
+            vmem(blocks, 8, width),
+            dma((3,)),
+            dma((3,)), dma((3,)),
+            dma((2,)), dma((1,)),
+            dma((2,)), dma((1,)),
+            dma((1,)), dma((1,)),
+            dma((1,)), dma((1,)),
+            dma((1,)), dma((blocks,)),
+            dma((1,)), dma((blocks,)),
         ],
         in_specs=[pl.BlockSpec(memory_space=pl.ANY)] * len(args),
         compiler_params=pltpu.CompilerParams(collective_id=0, has_side_effects=True),

time: 23.5 us -> 21.6 us (0.919)
  Pallas kernels: 22.6 us -> 20.8 us
    pallas_call x1, Pallas kernels: 21.9 us -> 20.1 us  [per_device(): pl.pallas_call(functools.partial(step_kernel, shape, nodes_dev), out_shap...]
where the time goes in v3:
time: 21.6 us; the launch traced here: 21.4 us
  Pallas kernels  20.8 us (96%)
  between operations  0.64 us (3%)
    pallas_call x1, Pallas kernels, per_device(): pl.pallas_call(functools.partial(step_kernel, shape, nodes_dev), out_shap...  20.1 us
    pallas_call x1, Pallas kernels, per_device(): pl.pallas_call(final_kernel, out_shape=tuple((jax.ShapeDtypeStruct(value....  0.68 us

profile of v3, /device:TPU:0, one launch (start us, length us, event | category | flops | bytes accessed | tf_op | source)
XLA Modules:
  0.0 21.4 jit_solution(15246703284970411926)
XLA Ops:
  0.6 20.1 %step.1 = (f32[24,128]{1,0:T(8,128)S(1)}, f32[3,96]{1,0:T(4,128)S(1)}, f32[6,2048]{1,0:T(8,128)S(1)}, f32[1,4]{1,0:T(1,128)S(1)}) custom-call(f32[24,128]{1,0:T(8,128)} %bitcast.18, f32[24,128]{1,0:T(8,128)} %bitcast.19, f32[5,24,128]{2,1,0:T(8,128)} %bitcast.15, s32[24,128]{1,0:T(8,128)} %bitcast.20, f32[5,32,128]{2,1,0:T(8,128)} %bitcast.13, ...), custom_call_target="tpu_custom_call" | custom-call | tf_op jit(solution)/shard_map/step/pallas_call | solution.py:720
  20.7 0.7 %final.1 = (f32[24,128]{1,0:T(8,128)}, f32[3,96]{1,0:T(4,128)}, f32[6,2048]{1,0:T(8,128)}, f32[1,4]{1,0:T(1,128)}) custom-call(f32[24,128]{1,0:T(8,128)S(1)} %get-tuple-element.12.refs_0_, f32[3,96]{1,0:T(4,128)S(1)} %get-tuple-element.13.refs_1_, f32[6,2048]{1,0:T(8,128)S(1)} %get-tuple-element.14.refs_2_, f32[1,4]{1,0:T(1,128)S(1)} %get-tuple-element.15.refs_3_), custom_call_target="tpu_custom_call" | custom-call | tf_op jit(solution)/shard_map/final/pallas_call | solution.py:760

commit v4 on v3

--- a/solution.py
+++ b/solution.py
@@ -162,8 +162,8 @@
     width = UNITS // blocks
     slots = width // HALF
     mats_rows = round_up(PAIRS + -(-(GPAR * (GPAR + 1) // 2) // slots), 8)
-    rhs_rows = round_up(CPAR + -(-GPAR // slots), 8)
     parts = width // LANES
+    rhs_rows = round_up(CPAR * parts + -(-GPAR // 2), 8)
     return plane, blocks, width, slots, mats_rows, rhs_rows, parts
 
 
@@ -206,11 +206,10 @@
     res_h, w_h, sp_h, si_h, sd_h, ap_h, ph_h, kn_h, cp_h, ci_h, gp_h,
     out_ref, step_ref, cstep_ref, glob_ref,
     res_ref, w_ref, sp_ref, si_ref, sd_ref, ap_ref, ph_ref, kn_ref, cp_ref, ci_ref, gp_ref,
-    first_ref, att, att_two, node_spots, unit_spots, cal, rcal, acc_att, acc_cal,
+    first_ref, att, unit_spots, cal, rcal, acc_att, acc_cal,
     normal_ref, mats_ref, rhs_ref,
     near, pmat, prhs, zmat, zrhs, solved_ref, solved_all, white_ref, white_all,
-    load_s, near_s, near_r, pmat_s, pmat_r, prhs_s, prhs_r,
-    zmat_s, zmat_r, zrhs_s, zrhs_r, solved_s, solved_r, white_s, white_r,
+    load_s, near_s, near_r, sent, pmat_r, prhs_r, zmat_r, zrhs_r, solved_r, white_r,
 ):
     count, groups, inner = shape
     plane, blocks, width, slots, mats_rows, rhs_rows, parts = layout(shape)
@@ -275,6 +274,7 @@
         greet(member(partner(m, k, plane)))
 
     loaded(0)
+    loaded(1)
     tiles = res_ref.shape[0]
     source_rows = sd_ref.shape[1]
     table = jnp.concatenate(
@@ -298,7 +298,6 @@
         total = jnp.sum(jnp.where(levels == high, total, 0.0), axis=0, keepdims=True)
         first_ref[tile : tile + 1, :] = res_ref[tile : tile + 1, :] - total[:, :LANES]
         first_ref[tile + 1 : tile + 2, :] = res_ref[tile + 1 : tile + 2, :] - total[:, LANES:]
-    loaded(1)
     weights = w_ref[...]
     first = first_ref[...]
     basis = spline_basis(ph_ref[...])
@@ -317,12 +316,11 @@
             att[place * tiles : (place + 1) * tiles, :] = basis[i_] * right
             place += 1
     base = t * (tiles * KPT)
-    for tile in range(tiles):
-        span = slice(tile * LANES, (tile + 1) * LANES)
-        value = att[pl.ds(tile, ATT_ROWS, stride=tiles), :]
-        att_two[:, span] = jnp.concatenate(split_two(value), axis=0)
-        node_spots[:, span] = one_hot(kn_ref[tile : tile + 1, :] - base, LANES)
-    sums = dot_nt(att_two[...], node_spots[...])
+    sums = None
+    for tile in range(0, tiles, 2):
+        lhs = jnp.concatenate(split_two(two_tiles(att, tile, ATT_ROWS, tiles)), axis=0)
+        part = dot_nt(lhs, one_hot(two_rows(kn_ref, tile) - base, LANES))
+        sums = part if sums is None else sums + part
     acc_att[...] = sums[:ATT_ROWS] + sums[ATT_ROWS:]
     band = [None] * 5
     place = 0
@@ -349,8 +347,8 @@
         return pltpu.make_async_remote_copy(
             src_ref=normal_ref,
             dst_ref=near.at[slot],
-            send_sem=near_s.at[offset + 1],
-            recv_sem=near_r.at[1 - offset],
+            send_sem=near_s.at[0],
+            recv_sem=near_r.at[0],
             device_id={"tm": t + offset, "grp": peer_grp(k)},
             device_id_type=MESH,
         )
@@ -369,17 +367,16 @@
         for k in range(1, groups):
             do(0, k)
 
-    def drain_near(sems):
-        @pl.when(has_before)
+    def drain_near(sem):
+        inside = jnp.logical_and(has_before, has_after)
+
+        @pl.when(inside)
         def _():
-            drain(near.at[0:groups], sems.at[0])
-
-        @pl.when(has_after)
+            drain(near.at[0 : 3 * groups - 1], sem)
+
+        @pl.when(jnp.logical_not(inside))
         def _():
-            drain(near.at[0:groups], sems.at[2])
-
-        if groups > 1:
-            drain(near.at[0 : groups - 1], sems.at[1])
+            drain(near.at[0 : 2 * groups - 1], sem)
 
     each_near(lambda offset, k: near_copy(offset, k).start())
 
@@ -403,7 +400,7 @@
         units = two_rows(ci_ref, tile)
         upper, lower = lax.shift_right_logical(units, 8), lax.bitwise_and(units, 255)
         spots = one_hot(lower, LOW)
-        unit_spots[no] = spots
+        unit_spots[no] = one_hot(lax.bitwise_and(units, LANES - 1), LANES)
         part = acc_cal[...]
         for piece in split_two(two_tiles(cal, tile, UNIT_ROWS, tiles)):
             part = part + dot_nt(by_high(piece.astype(F32), upper), spots)
@@ -422,13 +419,13 @@
             for j, piece in enumerate(pieces):
                 mats_ref[b_, PAIRS + no : PAIRS + no + 1, j * LANES : (j + 1) * LANES] = piece
 
-    def to_owners(source, target, send, recv):
+    def to_owners(source, target, recv):
         def copy(k):
             p = partner(block, k, blocks)
             pltpu.make_async_remote_copy(
                 src_ref=source.at[p],
                 dst_ref=target.at[m],
-                send_sem=send.at[min(k, 1)],
+                send_sem=sent.at[0],
                 recv_sem=recv.at[0],
                 device_id=member(2 * p + 1),
                 device_id_type=MESH,
@@ -445,19 +442,12 @@
         def _():
             target[m] = source[block]
 
-    def sent_to_owners(source, send):
-        drain(source.at[0 : blocks - 1], send.at[1])
-
-        @pl.when(follower)
-        def _():
-            drain(source.at[0:1], send.at[0])
-
-    def to_levels(target, send, recv):
+    def to_levels(target, recv):
         for k in range(1, depth):
             pltpu.make_async_remote_copy(
                 src_ref=target.at[z],
                 dst_ref=target.at[z],
-                send_sem=send.at[0],
+                send_sem=sent.at[0],
                 recv_sem=recv.at[0],
                 device_id=level(k),
                 device_id_type=MESH,
@@ -469,7 +459,7 @@
             out = out + buffer[k]
         return out
 
-    to_owners(mats_ref, pmat, pmat_s, pmat_r)
+    to_owners(mats_ref, pmat, pmat_r)
     near[groups + g] = normal_ref[...]
 
     @pl.when(jnp.logical_not(has_before))
@@ -480,7 +470,7 @@
     def _():
         near[2 * groups :] = jnp.zeros((groups, NORMAL_ROWS, LANES), F32)
 
-    drain_near(near_r)
+    drain_near(near_r.at[0])
     sums = []
     for s in range(3):
         part = near[s * groups]
@@ -512,6 +502,12 @@
     def precondition(vector):
         return solve_upper(lower, inverse, solve_lower(lower, inverse, vector))
 
+    turned = [
+        pltpu.roll(normals[d * 6 : (d + 1) * 6], d, 1) if d else None for d in range(4)
+    ]
+    behind = [
+        [turned[d][p : p + 1, :] for p in range(6)] if d else None for d in range(4)
+    ]
     x = [OMEGA * value for value in precondition(right)]
     for _ in range(1, ATT_SWEEPS):
         out = [right[c] - x[c] for c in range(3)]
@@ -521,11 +517,12 @@
                 for b in range(3):
                     out[a] = out[a] - band[d][index[a, b]] * ahead[b]
         for d in range(1, 4):
+            back = [pltpu.roll(x[c], d, 1) for c in range(3)]
             for a in range(3):
-                term = band[d][index[a, 0]] * x[0]
+                term = behind[d][index[a, 0]] * back[0]
                 for b in range(1, 3):
-                    term = term + band[d][index[a, b]] * x[b]
-                out[a] = out[a] - pltpu.roll(term, d, 1)
+                    term = term + behind[d][index[a, b]] * back[b]
+                out[a] = out[a] - term
         change = precondition(out)
         x = [jnp.where(exists, x[c] + OMEGA * change[c], 0.0) for c in range(3)]
 
@@ -541,28 +538,46 @@
     weighted = weights * second
     for a in range(CPAR):
         rcal[a * tiles : (a + 1) * tiles, :] = weighted * cp_ref[a]
-    rcal[CPAR * tiles :, :] = jnp.zeros(((8 - CPAR) * tiles, LANES), F32)
     global_rows = fold_slots(
-        [jnp.sum(weighted * gp_ref[a], axis=0, keepdims=True) for a in range(GPAR)], slots
-    )
+        [jnp.sum(weighted * gp_ref[a], axis=0, keepdims=True) for a in range(GPAR)], 2
+    )
+    unit_rows = lax.broadcasted_iota(jnp.int32, (CPAR * parts, 2 * LANES), 0)
+    level_of_row = lax.rem(unit_rows, parts)
     acc = None
     for no in range(tiles // 2):
         tile = no * 2
-        upper = lax.shift_right_logical(two_rows(ci_ref, tile), 8)
-        pieces = [
-            by_high(p.astype(F32), upper) for p in split_two(two_tiles(rcal, tile, 8, tiles))
-        ]
-        part = dot_nt(jnp.concatenate(pieces, axis=0), unit_spots[no])
+        upper = lax.shift_right_logical(two_rows(ci_ref, tile), 7)
+        value = None
+        for c in range(CPAR):
+            row = jnp.concatenate(
+                [
+                    rcal[c * tiles + tile : c * tiles + tile + 1, :],
+                    rcal[c * tiles + tile + 1 : c * tiles + tile + 2, :],
+                ],
+                axis=1,
+            )
+            row = jnp.broadcast_to(row, (CPAR * parts, 2 * LANES))
+            value = row if c == 0 else jnp.where(unit_rows >= c * parts, row, value)
+        lhs = jnp.concatenate(
+            [
+                jnp.where(level_of_row + b_ * parts == upper, piece.astype(F32), 0.0)
+                for piece in split_two(value)
+                for b_ in range(blocks)
+            ],
+            axis=0,
+        ).astype(BF16)
+        part = dot_nt(lhs, unit_spots[no])
         acc = part if acc is None else acc + part
-    rows = 8 * (UNITS // LOW)
-    total = acc[0:rows, :] + acc[rows : 2 * rows, :]
-    for b_, at, h, start in block_pieces(blocks):
-        rhs_ref[b_, 0:8, at : at + LANES] = total[h * 8 : h * 8 + 8, start : start + LANES]
+    rows = CPAR * parts
+    total = acc[0 : blocks * rows, :] + acc[blocks * rows :, :]
     for b_ in range(blocks):
+        rhs_ref[b_, 0:rows, :] = total[b_ * rows : (b_ + 1) * rows, :]
         for no, pieces in enumerate(global_rows):
-            for j, piece in enumerate(pieces):
-                rhs_ref[b_, CPAR + no : CPAR + no + 1, j * LANES : (j + 1) * LANES] = piece
-    to_owners(rhs_ref, prhs, prhs_s, prhs_r)
+            rhs_ref[b_, rows + no : rows + no + 1, :] = pieces[0]
+        first_free = rows + len(global_rows)
+        if first_free < rhs_rows:
+            rhs_ref[b_, first_free:, :] = jnp.zeros((rhs_rows - first_free, LANES), F32)
+    to_owners(rhs_ref, prhs, prhs_r)
 
     for c in range(3):
         scaled = lower[c][c] * x[c]
@@ -571,14 +586,14 @@
         moved = pltpu.roll(scaled, LANES - HALO, 1)
         step_ref[c : c + 1, :] = moved[:, 0:nodes_dev]
 
-    def spread(source, target, send, recv):
+    def spread(source, target, recv, shared):
         for p in reversed(range(1, plane)):
             to = partner(m, p, plane)
             pltpu.make_async_remote_copy(
                 src_ref=source,
                 dst_ref=target.at[block],
-                send_sem=send.at[0],
-                recv_sem=recv.at[p // 2],
+                send_sem=sent.at[0],
+                recv_sem=recv.at[0 if shared else p // 2],
                 device_id=member(to),
                 device_id_type=MESH,
             ).start()
@@ -587,11 +602,11 @@
     def _():
         drain(pmat.at[0 : plane - 1], pmat_r.at[0])
         zmat[z] = slots_total(pmat, plane)
-        to_levels(zmat, zmat_s, zmat_r)
+        to_levels(zmat, zmat_r)
 
         drain(prhs.at[0 : plane - 1], prhs_r.at[0])
         zrhs[z] = slots_total(prhs, plane)
-        to_levels(zrhs, zrhs_s, zrhs_r)
+        to_levels(zrhs, zrhs_r)
 
         drain(zmat.at[0 : depth - 1], zmat_r.at[0])
         unit_total = slots_total(zmat, depth)
@@ -604,33 +619,42 @@
 
         drain(zrhs.at[0 : depth - 1], zrhs_r.at[0])
         total = slots_total(zrhs, depth)
-        right = [total[c : c + 1, :] for c in range(CPAR)]
+        right = [
+            jnp.concatenate(
+                [total[c * parts + j : c * parts + j + 1, :] for j in range(parts)], axis=1
+            )
+            for c in range(CPAR)
+        ]
         white = solve_lower(lower, inverse, right)
         solved = solve_upper(lower, inverse, white)
         for c in range(CPAR):
             for j in range(parts):
                 row = c * parts + j
                 solved_ref[row : row + 1, :] = solved[c][:, j * LANES : (j + 1) * LANES]
-        spread(solved_ref, solved_all, solved_s, solved_r)
+        spread(solved_ref, solved_all, solved_r, False)
         for c in range(CPAR):
-            white_ref[c : c + 1, :] = white[c]
-        right_g = [slot_sum(total, CPAR, c, slots) for c in range(GPAR)]
+            for j in range(parts):
+                row = c * parts + j
+                white_ref[row : row + 1, :] = white[c][:, j * LANES : (j + 1) * LANES]
+        right_g = [slot_sum(total, CPAR * parts, c, 2) for c in range(GPAR)]
         white_g = solve_lower(lower_g, inverse_g, right_g)
         solved_g = solve_upper(lower_g, inverse_g, white_g)
-        white_ref[CPAR:, :] = jnp.zeros((8 - CPAR, width), F32)
         spot = lax.broadcasted_iota(jnp.int32, (1, LANES), 1)
         packed = jnp.zeros((1, LANES), F32)
         for c in range(GPAR):
             packed = jnp.where(spot == c, white_g[c], packed)
             packed = jnp.where(spot == GPAR + c, solved_g[c], packed)
-        white_ref[CPAR : CPAR + 1, 0:LANES] = packed
-        spread(white_ref, white_all, white_s, white_r)
+        white_ref[CPAR * parts : CPAR * parts + 1, :] = packed
+        spread(white_ref, white_all, white_r, True)
         solved_all[block] = solved_ref[...]
         white_all[block] = white_ref[...]
 
     units = ci_ref[...]
     high, low = lax.shift_right_logical(units, 7), lax.bitwise_and(units, 127)
-    picked = [jnp.zeros((tiles, LANES), F32) for _ in range(CPAR)]
+    slices = [(at, min(8, tiles - at)) for at in range(0, tiles, 8)]
+    highs = [high[at : at + size] for at, size in slices]
+    lows = [low[at : at + size] for at, size in slices]
+    picked = [[jnp.zeros((size, LANES), F32) for _, size in slices] for _ in range(CPAR)]
     for k in range(blocks):
         source = partner(block, k, blocks)
         if k:
@@ -639,44 +663,53 @@
             @pl.when(follower)
             def _():
                 drain(solved_ref, solved_r.at[0])
-        for j in range(parts):
-            here = high == source * parts + j
-            for c in range(CPAR):
-                row = c * parts + j
-                table = jnp.broadcast_to(
-                    solved_all[source, row : row + 1, :], (tiles, LANES)
-                )
-                picked[c] = jnp.where(here, lane_pick(table, low), picked[c])
+        for n, (_, size) in enumerate(slices):
+            for j in range(parts):
+                here = highs[n] == source * parts + j
+                for c in range(CPAR):
+                    row = c * parts + j
+                    table = jnp.broadcast_to(
+                        solved_all[source, row : row + 1, :], (size, LANES)
+                    )
+                    picked[c][n] = jnp.where(here, lane_pick(table, lows[n]), picked[c][n])
+    picked = [jnp.concatenate(rows, axis=0) for rows in picked]
     out = out_ref[...]
     for c in range(CPAR):
         out = out - cp_ref[c] * picked[c]
-    for k in range(blocks):
-        if k:
-            drain(white_ref, white_r.at[k])
-        else:
-            @pl.when(follower)
-            def _():
-                drain(white_ref, white_r.at[0])
+
+    @pl.when(owner)
+    def _():
+        drain(white_all.at[0 : blocks - 1], white_r.at[0])
+
+    @pl.when(follower)
+    def _():
+        drain(white_all, white_r.at[0])
+
     for b_ in range(blocks):
-        cstep_ref[:, b_ * width : (b_ + 1) * width] = white_all[b_, 0:CPAR, :]
-    packed = white_all[0, CPAR : CPAR + 1, 0:LANES]
+        for c in range(CPAR):
+            for j in range(parts):
+                start = b_ * width + j * LANES
+                row = c * parts + j
+                cstep_ref[c : c + 1, start : start + LANES] = white_all[b_, row : row + 1, :]
+    packed = white_all[0, CPAR * parts : CPAR * parts + 1, :]
     glob_ref[...] = packed[:, 0:GPAR]
     for c in range(GPAR):
         value = packed[:, GPAR + c : GPAR + c + 1]
         out = out - gp_ref[c] * jnp.broadcast_to(value, (1, LANES))
     out_ref[...] = out
-    drain_near(near_s)
-    sent_to_owners(mats_ref, pmat_s)
-    sent_to_owners(rhs_ref, prhs_s)
+    drain_near(near_s.at[0])
+    size = width // LANES * mats_rows + rhs_rows
 
     @pl.when(owner)
     def _():
-        drain(zmat.at[0 : depth - 1], zmat_s.at[0])
-        drain(zrhs.at[0 : depth - 1], zrhs_s.at[0])
-        size = (plane - 1) * math.prod(solved_ref.shape) // LANES
-        drain(att.at[0:size], solved_s.at[0])
-        size = (plane - 1) * math.prod(white_ref.shape) // LANES
-        drain(att.at[0:size], white_s.at[0])
+        ready = 2 * CPAR * parts + 1
+        drain(
+            att.at[0 : (blocks - 1 + depth - 1) * size + (plane - 1) * ready], sent.at[0]
+        )
+
+    @pl.when(follower)
+    def _():
+        drain(att.at[0 : blocks * size], sent.at[0])
 
 
 def final_kernel(*refs):
@@ -725,33 +758,26 @@
         scratch_shapes=[pltpu.VMEM(arg.shape, arg.dtype) for arg in args] + [
             vmem(tiles, LANES),
             vmem(ATT_ROWS * tiles, LANES),
-            pltpu.VMEM((2 * ATT_ROWS, row_count), BF16),
-            pltpu.VMEM((LANES, row_count), BF16),
-            pltpu.VMEM((tiles // 2, LOW, 2 * LANES), BF16),
+            pltpu.VMEM((tiles // 2, LANES, 2 * LANES), BF16),
             vmem(UNIT_ROWS * tiles, LANES),
-            vmem(8 * tiles, LANES),
+            vmem(CPAR * tiles, LANES),
             vmem(ATT_ROWS, LANES),
             vmem(UNIT_ROWS * (UNITS // LOW), LOW),
             vmem(NORMAL_ROWS, LANES),
             vmem(blocks, mats_rows, width),
-            vmem(blocks, rhs_rows, width),
+            vmem(blocks, rhs_rows, LANES),
             vmem(3 * groups, NORMAL_ROWS, LANES),
             vmem(plane, mats_rows, width),
-            vmem(plane, rhs_rows, width),
+            vmem(plane, rhs_rows, LANES),
             vmem(depth, mats_rows, width),
-            vmem(depth, rhs_rows, width),
+            vmem(depth, rhs_rows, LANES),
             vmem(CPAR * parts, LANES),
             vmem(blocks, CPAR * parts, LANES),
-            vmem(8, width),
-            vmem(blocks, 8, width),
-            dma((3,)),
-            dma((3,)), dma((3,)),
-            dma((2,)), dma((1,)),
-            dma((2,)), dma((1,)),
-            dma((1,)), dma((1,)),
-            dma((1,)), dma((1,)),
-            dma((1,)), dma((blocks,)),
-            dma((1,)), dma((blocks,)),
+            vmem(CPAR * parts + 1, LANES),
+            vmem(blocks, CPAR * parts + 1, LANES),
+            dma((3,)), dma((1,)), dma((1,)), dma((1,)),
+            dma((1,)), dma((1,)), dma((1,)), dma((1,)),
+            dma((blocks,)), dma((1,)),
         ],
         in_specs=[pl.BlockSpec(memory_space=pl.ANY)] * len(args),
         compiler_params=pltpu.CompilerParams(collective_id=0, has_side_effects=True),

time: 21.6 us -> 21 us (0.972)
  Pallas kernels: 20.8 us -> 20.2 us
    pallas_call x1, Pallas kernels: 20.1 us -> 19.5 us  [per_device(): pl.pallas_call(functools.partial(step_kernel, shape, nodes_dev), out_shap...]
where the time goes in v4:
time: 21 us; the launch traced here: 20.8 us
  Pallas kernels  20.2 us (96%)
  between operations  0.64 us (3%)
    pallas_call x1, Pallas kernels, per_device(): pl.pallas_call(functools.partial(step_kernel, shape, nodes_dev), out_shap...  19.5 us
    pallas_call x1, Pallas kernels, per_device(): pl.pallas_call(final_kernel, out_shape=tuple((jax.ShapeDtypeStruct(value....  0.68 us

profile of v4, /device:TPU:0, one launch (start us, length us, event | category | flops | bytes accessed | tf_op | source)
XLA Modules:
  0.0 20.8 jit_solution(9591228837284920232)
XLA Ops:
  0.6 19.5 %step.1 = (f32[24,128]{1,0:T(8,128)S(1)}, f32[3,96]{1,0:T(4,128)S(1)}, f32[6,2048]{1,0:T(8,128)S(1)}, f32[1,4]{1,0:T(1,128)S(1)}) custom-call(f32[24,128]{1,0:T(8,128)} %bitcast.18, f32[24,128]{1,0:T(8,128)} %bitcast.19, f32[5,24,128]{2,1,0:T(8,128)} %bitcast.15, s32[24,128]{1,0:T(8,128)} %bitcast.20, f32[5,32,128]{2,1,0:T(8,128)} %bitcast.13, ...), custom_call_target="tpu_custom_call" | custom-call | tf_op jit(solution)/shard_map/step/pallas_call | solution.py:753
  20.1 0.7 %final.1 = (f32[24,128]{1,0:T(8,128)}, f32[3,96]{1,0:T(4,128)}, f32[6,2048]{1,0:T(8,128)}, f32[1,4]{1,0:T(1,128)}) custom-call(f32[24,128]{1,0:T(8,128)S(1)} %get-tuple-element.12.refs_0_, f32[3,96]{1,0:T(4,128)S(1)} %get-tuple-element.13.refs_1_, f32[6,2048]{1,0:T(8,128)S(1)} %get-tuple-element.14.refs_2_, f32[1,4]{1,0:T(1,128)S(1)} %get-tuple-element.15.refs_3_), custom_call_target="tpu_custom_call" | custom-call | tf_op jit(solution)/shard_map/final/pallas_call | solution.py:786

commit v5 on v4

--- a/solution.py
+++ b/solution.py
@@ -79,6 +79,15 @@
                 entry = entry - lower[row][k] * lower[column][k]
             lower[row][column] = entry * inverse[column]
     return lower, inverse
+
+
+def tree_sum(values):
+    while len(values) > 1:
+        values = [
+            values[k] + values[k + 1] if k + 1 < len(values) else values[k]
+            for k in range(0, len(values), 2)
+        ]
+    return values[0]
 
 
 def solve_lower(lower, inverse, vector):
@@ -250,7 +259,7 @@
         return {"tm": z * inner + lax.rem(p, inner), "grp": lax.div(p, inner)}
 
     def level(k):
-        return {"tm": lax.rem(t + k * inner, count), "grp": g}
+        return {"tm": partner(z, k, depth) * inner + i, "grp": g}
 
     barrier = pltpu.get_barrier_semaphore()
 
@@ -354,6 +363,9 @@
         )
 
     def each_near(do):
+        for k in range(1, groups):
+            do(0, k)
+
         @pl.when(has_before)
         def _():
             for k in reversed(range(groups)):
@@ -363,9 +375,6 @@
         def _():
             for k in reversed(range(groups)):
                 do(1, k)
-
-        for k in range(1, groups):
-            do(0, k)
 
     def drain_near(sem):
         inside = jnp.logical_and(has_before, has_after)
@@ -399,19 +408,24 @@
         tile = no * 2
         units = two_rows(ci_ref, tile)
         upper, lower = lax.shift_right_logical(units, 8), lax.bitwise_and(units, 255)
-        spots = one_hot(lower, LOW)
-        unit_spots[no] = one_hot(lax.bitwise_and(units, LANES - 1), LANES)
-        part = acc_cal[...]
-        for piece in split_two(two_tiles(cal, tile, UNIT_ROWS, tiles)):
-            part = part + dot_nt(by_high(piece.astype(F32), upper), spots)
-        acc_cal[...] = part
+        lhs = jnp.concatenate(
+            [
+                by_high(piece.astype(F32), upper)
+                for piece in split_two(two_tiles(cal, tile, UNIT_ROWS, tiles))
+            ],
+            axis=0,
+        )
+        acc_cal[...] = acc_cal[...] + dot_nt(lhs, one_hot(lower, LOW))
         return carry
 
     lax.fori_loop(0, tiles // 2, bin_units, 0, unroll=6)
+    lo_rows = UNIT_ROWS * (UNITS // LOW)
     for b_, at, h, start in block_pieces(blocks):
-        mats_ref[b_, 0:UNIT_ROWS, at : at + LANES] = acc_cal[
-            h * UNIT_ROWS : (h + 1) * UNIT_ROWS, start : start + LANES
-        ]
+        row = h * UNIT_ROWS
+        mats_ref[b_, 0:UNIT_ROWS, at : at + LANES] = (
+            acc_cal[row : row + UNIT_ROWS, start : start + LANES]
+            + acc_cal[lo_rows + row : lo_rows + row + UNIT_ROWS, start : start + LANES]
+        )
     if mats_rows > UNIT_ROWS:
         mats_ref[:, UNIT_ROWS:, :] = jnp.zeros((blocks, mats_rows - UNIT_ROWS, width), F32)
     for b_ in range(blocks):
@@ -442,8 +456,8 @@
         def _():
             target[m] = source[block]
 
-    def to_levels(target, recv):
-        for k in range(1, depth):
+    def to_levels(target, recv, ks):
+        for k in ks:
             pltpu.make_async_remote_copy(
                 src_ref=target.at[z],
                 dst_ref=target.at[z],
@@ -460,6 +474,10 @@
         return out
 
     to_owners(mats_ref, pmat, pmat_r)
+    for no in range(tiles // 2):
+        unit_spots[no] = one_hot(
+            lax.bitwise_and(two_rows(ci_ref, no * 2), LANES - 1), LANES
+        )
     near[groups + g] = normal_ref[...]
 
     @pl.when(jnp.logical_not(has_before))
@@ -499,8 +517,19 @@
     right = [normals[24 + c : 25 + c, :] for c in range(3)]
     lower, inverse = cholesky_lists(symmetric(band[0], 3), 3)
 
+    low = [
+        [inverse[0]],
+        [-lower[1][0] * inverse[0] * inverse[1], inverse[1]],
+        [None, -lower[2][1] * inverse[1] * inverse[2], inverse[2]],
+    ]
+    low[2][0] = -(lower[2][0] * low[0][0] + lower[2][1] * low[1][0]) * inverse[2]
+    damped = {}
+    for a, b in pairs_of(3):
+        entry = tree_sum([low[k][a] * low[k][b] for k in range(b, 3)])
+        damped[a, b] = damped[b, a] = OMEGA * entry
+
     def precondition(vector):
-        return solve_upper(lower, inverse, solve_lower(lower, inverse, vector))
+        return [tree_sum([damped[a, b] * vector[b] for b in range(3)]) for a in range(3)]
 
     turned = [
         pltpu.roll(normals[d * 6 : (d + 1) * 6], d, 1) if d else None for d in range(4)
@@ -508,23 +537,23 @@
     behind = [
         [turned[d][p : p + 1, :] for p in range(6)] if d else None for d in range(4)
     ]
-    x = [OMEGA * value for value in precondition(right)]
+    x = precondition(right)
     for _ in range(1, ATT_SWEEPS):
-        out = [right[c] - x[c] for c in range(3)]
-        for d in range(4):
-            ahead = [pltpu.roll(x[c], LANES - d, 1) for c in range(3)] if d else x
+        out = [
+            right[a] - x[a] - tree_sum([band[0][index[a, b]] * x[b] for b in range(3)])
+            for a in range(3)
+        ]
+        terms = [[] for _ in range(3)]
+        for d in range(1, 4):
+            ahead = [pltpu.roll(x[c], LANES - d, 1) for c in range(3)]
+            back = [pltpu.roll(x[c], d, 1) for c in range(3)]
             for a in range(3):
                 for b in range(3):
-                    out[a] = out[a] - band[d][index[a, b]] * ahead[b]
-        for d in range(1, 4):
-            back = [pltpu.roll(x[c], d, 1) for c in range(3)]
-            for a in range(3):
-                term = behind[d][index[a, 0]] * back[0]
-                for b in range(1, 3):
-                    term = term + behind[d][index[a, b]] * back[b]
-                out[a] = out[a] - term
+                    terms[a].append(band[d][index[a, b]] * ahead[b])
+                    terms[a].append(behind[d][index[a, b]] * back[b])
+        out = [out[a] - tree_sum(terms[a]) for a in range(3)]
         change = precondition(out)
-        x = [jnp.where(exists, x[c] + OMEGA * change[c], 0.0) for c in range(3)]
+        x = [jnp.where(exists, x[c] + change[c], 0.0) for c in range(3)]
 
     local = kn_ref[...] - base + HALO
     tables = [jnp.broadcast_to(x[c], (tiles, LANES)) for c in range(3)]
@@ -602,11 +631,11 @@
     def _():
         drain(pmat.at[0 : plane - 1], pmat_r.at[0])
         zmat[z] = slots_total(pmat, plane)
-        to_levels(zmat, zmat_r)
+        to_levels(zmat, zmat_r, reversed(range(1, depth)))
 
         drain(prhs.at[0 : plane - 1], prhs_r.at[0])
         zrhs[z] = slots_total(prhs, plane)
-        to_levels(zrhs, zrhs_r)
+        to_levels(zrhs, zrhs_r, reversed(range(1, depth)))
 
         drain(zmat.at[0 : depth - 1], zmat_r.at[0])
         unit_total = slots_total(zmat, depth)
@@ -762,7 +791,7 @@
             vmem(UNIT_ROWS * tiles, LANES),
             vmem(CPAR * tiles, LANES),
             vmem(ATT_ROWS, LANES),
-            vmem(UNIT_ROWS * (UNITS // LOW), LOW),
+            vmem(2 * UNIT_ROWS * (UNITS // LOW), LOW),
             vmem(NORMAL_ROWS, LANES),
             vmem(blocks, mats_rows, width),
             vmem(blocks, rhs_rows, LANES),

time: 21 us -> 20.6 us (0.981)
  Pallas kernels: 20.2 us -> 19.8 us
    pallas_call x1, Pallas kernels: 19.5 us -> 19.1 us  [per_device(): pl.pallas_call(functools.partial(step_kernel, shape, nodes_dev), out_shap...]
where the time goes in v5:
time: 20.6 us; the launch traced here: 20.4 us
  Pallas kernels  19.8 us (96%)
  between operations  0.64 us (3%)
    pallas_call x1, Pallas kernels, per_device(): pl.pallas_call(functools.partial(step_kernel, shape, nodes_dev), out_shap...  19.1 us
    pallas_call x1, Pallas kernels, per_device(): pl.pallas_call(final_kernel, out_shape=tuple((jax.ShapeDtypeStruct(value....  0.68 us

profile of v5, /device:TPU:0, one launch (start us, length us, event | category | flops | bytes accessed | tf_op | source)
XLA Modules:
  0.0 20.4 jit_solution(6965064289975890464)
XLA Ops:
  0.6 19.1 %step.1 = (f32[24,128]{1,0:T(8,128)S(1)}, f32[3,96]{1,0:T(4,128)S(1)}, f32[6,2048]{1,0:T(8,128)S(1)}, f32[1,4]{1,0:T(1,128)S(1)}) custom-call(f32[24,128]{1,0:T(8,128)} %bitcast.18, f32[24,128]{1,0:T(8,128)} %bitcast.19, f32[5,24,128]{2,1,0:T(8,128)} %bitcast.15, s32[24,128]{1,0:T(8,128)} %bitcast.20, f32[5,32,128]{2,1,0:T(8,128)} %bitcast.13, ...), custom_call_target="tpu_custom_call" | custom-call | tf_op jit(solution)/shard_map/step/pallas_call | solution.py:782
  19.7 0.7 %final.1 = (f32[24,128]{1,0:T(8,128)}, f32[3,96]{1,0:T(4,128)}, f32[6,2048]{1,0:T(8,128)}, f32[1,4]{1,0:T(1,128)}) custom-call(f32[24,128]{1,0:T(8,128)S(1)} %get-tuple-element.12.refs_0_, f32[3,96]{1,0:T(4,128)S(1)} %get-tuple-element.13.refs_1_, f32[6,2048]{1,0:T(8,128)S(1)} %get-tuple-element.14.refs_2_, f32[1,4]{1,0:T(1,128)S(1)} %get-tuple-element.15.refs_3_), custom_call_target="tpu_custom_call" | custom-call | tf_op jit(solution)/shard_map/final/pallas_call | solution.py:815

commit v6 on v5

--- a/solution.py
+++ b/solution.py
@@ -172,7 +172,7 @@
     slots = width // HALF
     mats_rows = round_up(PAIRS + -(-(GPAR * (GPAR + 1) // 2) // slots), 8)
     parts = width // LANES
-    rhs_rows = round_up(CPAR * parts + -(-GPAR // 2), 8)
+    rhs_rows = CPAR * parts + -(-GPAR // 2)
     return plane, blocks, width, slots, mats_rows, rhs_rows, parts
 
 
@@ -215,7 +215,7 @@
     res_h, w_h, sp_h, si_h, sd_h, ap_h, ph_h, kn_h, cp_h, ci_h, gp_h,
     out_ref, step_ref, cstep_ref, glob_ref,
     res_ref, w_ref, sp_ref, si_ref, sd_ref, ap_ref, ph_ref, kn_ref, cp_ref, ci_ref, gp_ref,
-    first_ref, att, unit_spots, cal, rcal, acc_att, acc_cal,
+    first_ref, att, by_node, unit_spots, cal, rcal, acc_att, acc_cal,
     normal_ref, mats_ref, rhs_ref,
     near, pmat, prhs, zmat, zrhs, solved_ref, solved_all, white_ref, white_all,
     load_s, near_s, near_r, sent, pmat_r, prhs_r, zmat_r, zrhs_r, solved_r, white_r,
@@ -325,12 +325,15 @@
             att[place * tiles : (place + 1) * tiles, :] = basis[i_] * right
             place += 1
     base = t * (tiles * KPT)
-    sums = None
+    by_node[...] = jnp.zeros_like(by_node)
     for tile in range(0, tiles, 2):
-        lhs = jnp.concatenate(split_two(two_tiles(att, tile, ATT_ROWS, tiles)), axis=0)
-        part = dot_nt(lhs, one_hot(two_rows(kn_ref, tile) - base, LANES))
-        sums = part if sums is None else sums + part
-    acc_att[...] = sums[:ATT_ROWS] + sums[ATT_ROWS:]
+        spots = one_hot(two_rows(kn_ref, tile) - (base + tile * KPT), 16)
+        part = None
+        for piece in split_two(two_tiles(att, tile, ATT_ROWS, tiles)):
+            term = dot_nt(spots, piece)
+            part = term if part is None else part + term
+        by_node[tile * KPT : (tile + 2) * KPT, 0:ATT_ROWS] = part[0 : 2 * KPT, :]
+    acc_att[...] = jnp.transpose(by_node[...])[0:ATT_ROWS, :]
     band = [None] * 5
     place = 0
     for i_ in range(4):
@@ -354,8 +357,8 @@
     def near_copy(offset, k):
         slot = (1 - offset) * groups + g
         return pltpu.make_async_remote_copy(
-            src_ref=normal_ref,
-            dst_ref=near.at[slot],
+            src_ref=normal_ref.at[0:27],
+            dst_ref=near.at[slot, 0:27],
             send_sem=near_s.at[0],
             recv_sem=near_r.at[0],
             device_id={"tm": t + offset, "grp": peer_grp(k)},
@@ -381,11 +384,11 @@
 
         @pl.when(inside)
         def _():
-            drain(near.at[0 : 3 * groups - 1], sem)
+            drain(att.at[0 : 27 * (3 * groups - 1)], sem)
 
         @pl.when(jnp.logical_not(inside))
         def _():
-            drain(near.at[0 : 2 * groups - 1], sem)
+            drain(att.at[0 : 27 * (2 * groups - 1)], sem)
 
     each_near(lambda offset, k: near_copy(offset, k).start())
 
@@ -456,16 +459,27 @@
         def _():
             target[m] = source[block]
 
-    def to_levels(target, recv, ks):
-        for k in ks:
-            pltpu.make_async_remote_copy(
-                src_ref=target.at[z],
-                dst_ref=target.at[z],
-                send_sem=sent.at[0],
-                recv_sem=recv.at[0],
-                device_id=level(k),
-                device_id_type=MESH,
-            ).start()
+    def to_levels(target, recv, chosen):
+        for k in range(depth):
+            @pl.when(chosen(k))
+            def _():
+                pltpu.make_async_remote_copy(
+                    src_ref=target.at[z],
+                    dst_ref=target.at[z],
+                    send_sem=sent.at[0],
+                    recv_sem=recv.at[0],
+                    device_id={"tm": k * inner + i, "grp": g},
+                    device_id_type=MESH,
+                ).start()
+
+    def other(k):
+        return z != k
+
+    def late(k):
+        return z - k > 1 if k else z < 0
+
+    def soon(k):
+        return jnp.logical_and(other(k), jnp.logical_not(late(k)))
 
     def slots_total(buffer, number):
         out = buffer[0]
@@ -631,11 +645,12 @@
     def _():
         drain(pmat.at[0 : plane - 1], pmat_r.at[0])
         zmat[z] = slots_total(pmat, plane)
-        to_levels(zmat, zmat_r, reversed(range(1, depth)))
+        to_levels(zmat, zmat_r, soon)
 
         drain(prhs.at[0 : plane - 1], prhs_r.at[0])
         zrhs[z] = slots_total(prhs, plane)
-        to_levels(zrhs, zrhs_r, reversed(range(1, depth)))
+        to_levels(zrhs, zrhs_r, other)
+        to_levels(zmat, zmat_r, late)
 
         drain(zmat.at[0 : depth - 1], zmat_r.at[0])
         unit_total = slots_total(zmat, depth)
@@ -787,6 +802,7 @@
         scratch_shapes=[pltpu.VMEM(arg.shape, arg.dtype) for arg in args] + [
             vmem(tiles, LANES),
             vmem(ATT_ROWS * tiles, LANES),
+            vmem(LANES, LANES),
             pltpu.VMEM((tiles // 2, LANES, 2 * LANES), BF16),
             vmem(UNIT_ROWS * tiles, LANES),
             vmem(CPAR * tiles, LANES),

time: 20.6 us -> 20.2 us (0.981)
  Pallas kernels: 19.8 us -> 19.4 us
    pallas_call x1, Pallas kernels: 19.1 us -> 18.7 us  [per_device(): pl.pallas_call(functools.partial(step_kernel, shape, nodes_dev), out_shap...]
where the time goes in v6:
time: 20.2 us; the launch traced here: 20.1 us
  Pallas kernels  19.4 us (96%)
  between operations  0.64 us (3%)
    pallas_call x1, Pallas kernels, per_device(): pl.pallas_call(functools.partial(step_kernel, shape, nodes_dev), out_shap...  18.7 us
    pallas_call x1, Pallas kernels, per_device(): pl.pallas_call(final_kernel, out_shape=tuple((jax.ShapeDtypeStruct(value....  0.68 us

profile of v6, /device:TPU:0, one launch (start us, length us, event | category | flops | bytes accessed | tf_op | source)
XLA Modules:
  0.0 20.1 jit_solution(11842516743048660253)
XLA Ops:
  0.6 18.7 %step.1 = (f32[24,128]{1,0:T(8,128)S(1)}, f32[3,96]{1,0:T(4,128)S(1)}, f32[6,2048]{1,0:T(8,128)S(1)}, f32[1,4]{1,0:T(1,128)S(1)}) custom-call(f32[24,128]{1,0:T(8,128)} %bitcast.18, f32[24,128]{1,0:T(8,128)} %bitcast.19, f32[5,24,128]{2,1,0:T(8,128)} %bitcast.15, s32[24,128]{1,0:T(8,128)} %bitcast.20, f32[5,32,128]{2,1,0:T(8,128)} %bitcast.13, ...), custom_call_target="tpu_custom_call" | custom-call | tf_op jit(solution)/shard_map/step/pallas_call | solution.py:797
  19.4 0.7 %final.1 = (f32[24,128]{1,0:T(8,128)}, f32[3,96]{1,0:T(4,128)}, f32[6,2048]{1,0:T(8,128)}, f32[1,4]{1,0:T(1,128)}) custom-call(f32[24,128]{1,0:T(8,128)S(1)} %get-tuple-element.12.refs_0_, f32[3,96]{1,0:T(4,128)S(1)} %get-tuple-element.13.refs_1_, f32[6,2048]{1,0:T(8,128)S(1)} %get-tuple-element.14.refs_2_, f32[1,4]{1,0:T(1,128)S(1)} %get-tuple-element.15.refs_3_), custom_call_target="tpu_custom_call" | custom-call | tf_op jit(solution)/shard_map/final/pallas_call | solution.py:831

commit v7 on v6

--- a/solution.py
+++ b/solution.py
@@ -630,16 +630,19 @@
         step_ref[c : c + 1, :] = moved[:, 0:nodes_dev]
 
     def spread(source, target, recv, shared):
-        for p in reversed(range(1, plane)):
-            to = partner(m, p, plane)
-            pltpu.make_async_remote_copy(
-                src_ref=source,
-                dst_ref=target.at[block],
-                send_sem=sent.at[0],
-                recv_sem=recv.at[0 if shared else p // 2],
-                device_id=member(to),
-                device_id_type=MESH,
-            ).start()
+        for k in range(plane):
+            slot = 0 if shared else partner(block, k // 2, blocks)
+
+            @pl.when(m != k)
+            def _():
+                pltpu.make_async_remote_copy(
+                    src_ref=source,
+                    dst_ref=target.at[block],
+                    send_sem=sent.at[0],
+                    recv_sem=recv.at[slot],
+                    device_id={"tm": z * inner + k % inner, "grp": k // inner},
+                    device_id_type=MESH,
+                ).start()
 
     @pl.when(owner)
     def _():

time: 20.2 us -> 20.2 us (level)
  no operation moved by 1% of the time
where the time goes in v7:
time: 20.2 us; the launch traced here: 20.1 us
  Pallas kernels  19.4 us (96%)
  between operations  0.64 us (3%)
    pallas_call x1, Pallas kernels, per_device(): pl.pallas_call(functools.partial(step_kernel, shape, nodes_dev), out_shap...  18.7 us
    pallas_call x1, Pallas kernels, per_device(): pl.pallas_call(final_kernel, out_shape=tuple((jax.ShapeDtypeStruct(value....  0.68 us

profile of v7, /device:TPU:0, one launch (start us, length us, event | category | flops | bytes accessed | tf_op | source)
XLA Modules:
  0.0 20.1 jit_solution(4900902171149515741)
XLA Ops:
  0.6 18.7 %step.1 = (f32[24,128]{1,0:T(8,128)S(1)}, f32[3,96]{1,0:T(4,128)S(1)}, f32[6,2048]{1,0:T(8,128)S(1)}, f32[1,4]{1,0:T(1,128)S(1)}) custom-call(f32[24,128]{1,0:T(8,128)} %bitcast.18, f32[24,128]{1,0:T(8,128)} %bitcast.19, f32[5,24,128]{2,1,0:T(8,128)} %bitcast.15, s32[24,128]{1,0:T(8,128)} %bitcast.20, f32[5,32,128]{2,1,0:T(8,128)} %bitcast.13, ...), custom_call_target="tpu_custom_call" | custom-call | tf_op jit(solution)/shard_map/step/pallas_call | solution.py:800
  19.4 0.7 %final.1 = (f32[24,128]{1,0:T(8,128)}, f32[3,96]{1,0:T(4,128)}, f32[6,2048]{1,0:T(8,128)}, f32[1,4]{1,0:T(1,128)}) custom-call(f32[24,128]{1,0:T(8,128)S(1)} %get-tuple-element.12.refs_0_, f32[3,96]{1,0:T(4,128)S(1)} %get-tuple-element.13.refs_1_, f32[6,2048]{1,0:T(8,128)S(1)} %get-tuple-element.14.refs_2_, f32[1,4]{1,0:T(1,128)S(1)} %get-tuple-element.15.refs_3_), custom_call_target="tpu_custom_call" | custom-call | tf_op jit(solution)/shard_map/final/pallas_call | solution.py:834
